TPU v7x, 8 devices: a whole 2x2x1 slice. The times are simulated.
8 devices in a mesh: replica: 1 (over z), yz: 2 (over y), x: 4 (over x, core).
Axes of the slice: x: 2, y: 2, z: 1, core: 2. Of those that a mesh axis runs over, the one named last changes fastest.
Arguments:
- hidden: bfloat16 [512, 4096], P('replica', ('x', 'yz'))
- seq_lens: int32 [512], P(('replica', 'yz', 'x'))
- attn_gain: bfloat16 [1, 4096], replicated
- mlp_gain: bfloat16 [1, 4096], replicated
- w_qkv: bfloat16 [1, 4096, 4352], P(None, None, 'yz')
- w_out: bfloat16 [1, 4096, 4096], P(None, 'yz')
- w_gate_up: bfloat16 [1, 4096, 2, 14336], P(None, None, None, 'yz')
- w_down: bfloat16 [1, 14336, 4096], P(None, 'yz')
- k_cache: bfloat16 [1, 512, 2048, 128], P(None, ('replica', 'yz', 'x'))
- v_cache: bfloat16 [1, 512, 2048, 128], P(None, ('replica', 'yz', 'x'))
Outputs:
- output 1: bfloat16 [512, 4096], P('replica', ('x', 'yz'))
- output 2: bfloat16 [1, 512, 2048, 128], P(None, ('replica', 'yz', 'x'))
- output 3: bfloat16 [1, 512, 2048, 128], P(None, ('replica', 'yz', 'x'))
All inputs are finite; a program needn't handle non-finite values.
Results may differ from a plain program's by a relative error of at most 0.0136421.
Values are sent between devices in bfloat16 or wider.
A program may use at most 1.5 GiB of HBM per device.

v0:
```python
import jax
import jax.numpy as jnp
from jax import lax
from jax.sharding import PartitionSpec as P

NORM_EPS = 1e-5


def attend(z_rows, k_layer, v_layer, seq_lens, head_dim):
    num_rows = z_rows.shape[0]
    attn_width = z_rows.shape[1] - 2 * head_dim
    num_heads = attn_width // head_dim
    queries = z_rows[:, :attn_width].reshape(num_rows, num_heads, head_dim)
    k_new = z_rows[:, attn_width:attn_width + head_dim]
    v_new = z_rows[:, attn_width + head_dim:]
    slot_ids = jnp.arange(k_layer.shape[1])
    at_slot = (slot_ids[None, :] == seq_lens[:, None])[:, :, None]
    k_upd = jnp.where(at_slot, k_new[:, None, :], k_layer)
    v_upd = jnp.where(at_slot, v_new[:, None, :], v_layer)
    scores = jnp.einsum('bhd,bsd->bhs', queries, k_upd, preferred_element_type=jnp.float32) * head_dim ** -0.5
    visible = (slot_ids[None, :] <= seq_lens[:, None])[:, None, :]
    scores = jnp.where(visible, scores, -1e30)
    probs_bf = jax.nn.softmax(scores, axis=-1).astype(jnp.bfloat16)
    outputs = jnp.einsum('bhs,bsd->bhd', probs_bf, v_upd, preferred_element_type=jnp.float32)
    return outputs.astype(jnp.bfloat16).reshape(num_rows, attn_width), k_upd, v_upd


def solution(mesh):
    group_axes = ('yz', 'x')
    batch_axes = ('replica', 'yz', 'x')
    hidden_spec = P('replica', ('x', 'yz'))
    cache_spec = P(None, batch_axes, None, None)
    x_size = mesh.shape['x']

    def norm_part(h_part, gain_part, model_dim):
        hid_f = h_part.astype(jnp.float32)
        sq_power = lax.psum(jnp.sum(hid_f * hid_f, axis=1, keepdims=True), 'x')
        inv_scale = lax.rsqrt(sq_power / model_dim + NORM_EPS)
        return (hid_f * inv_scale * gain_part.astype(jnp.float32)).astype(jnp.bfloat16)

    def residual(hidden, partial_sum):
        summed = lax.psum_scatter(partial_sum.astype(jnp.bfloat16), 'yz', scatter_dimension=1, tiled=True)
        return (hidden.astype(jnp.float32) + summed.astype(jnp.float32)).astype(jnp.bfloat16)

    def local_step(hidden, seq_lens, attn_gain, mlp_gain, w_qkv, w_out, w_gate_up, w_down, k_cache, v_cache):
        head_dim = k_cache.shape[-1]
        model_dim = attn_gain.shape[1] * x_size
        k_layers = []
        v_layers = []
        for layer_idx in range(w_qkv.shape[0]):
            gathered = lax.all_gather(hidden, 'yz', axis=1, tiled=True)
            normed = norm_part(gathered, attn_gain[layer_idx], model_dim)
            partial_z = jnp.dot(normed, w_qkv[layer_idx], preferred_element_type=jnp.float32).astype(jnp.bfloat16)
            z_cols = lax.psum_scatter(partial_z, 'x', scatter_dimension=1, tiled=True)
            z_rows = lax.all_to_all(z_cols, group_axes, 0, 1, tiled=True)
            attn_rows, k_upd, v_upd = attend(z_rows, k_cache[layer_idx], v_cache[layer_idx], seq_lens, head_dim)
            k_layers.append(k_upd)
            v_layers.append(v_upd)
            attn_cols = lax.all_to_all(attn_rows, group_axes, 1, 0, tiled=True)
            attn_slab = lax.all_gather(attn_cols, 'x', axis=1, tiled=True)
            hidden = residual(hidden, jnp.dot(attn_slab, w_out[layer_idx], preferred_element_type=jnp.float32))
            gathered = lax.all_gather(hidden, 'yz', axis=1, tiled=True)
            normed = norm_part(gathered, mlp_gain[layer_idx], model_dim)
            gu_part = jnp.einsum('be,etf->btf', normed, w_gate_up[layer_idx], preferred_element_type=jnp.float32).astype(jnp.bfloat16)
            gu_cols = lax.psum_scatter(gu_part, 'x', scatter_dimension=2, tiled=True)
            mlp_cols = (jax.nn.silu(gu_cols[:, 0].astype(jnp.float32)) * gu_cols[:, 1].astype(jnp.float32)).astype(jnp.bfloat16)
            mlp_slab = lax.all_gather(mlp_cols, 'x', axis=1, tiled=True)
            hidden = residual(hidden, jnp.dot(mlp_slab, w_down[layer_idx], preferred_element_type=jnp.float32))
        return hidden, jnp.stack(k_layers), jnp.stack(v_layers)

    return jax.shard_map(
        local_step,
        mesh=mesh,
        in_specs=(hidden_spec, P(batch_axes), P(None, 'x'), P(None, 'x'), P(None, 'x', 'yz'), P(None, 'yz', 'x'),
                  P(None, 'x', None, 'yz'), P(None, 'yz', 'x'), cache_spec, cache_spec),
        out_specs=(hidden_spec, cache_spec, cache_spec),
        check_vma=False)
```

profile of v0, /device:TPU:0, one launch (start us, length us, event | category | flops | bytes accessed | tf_op | source)
XLA Modules:
  0.0 502.7 jit_solution(9350746582420733805)
XLA Ops:
  7.2 0.0 copy-start.2
  7.2 0.0 all-gather.5.cloned.1.call-start
  7.2 0.7 all-gather.5.cloned.1.call-update
  7.9 0.0 reduce-scatter.5.cloned.1.call-start
  8.0 1.2 dynamic-slice.7
  9.2 1.2 dynamic-slice
  11.1 0.7 dynamic-slice_convert_fusion.1
  11.8 18.9 %all-gather.5.cloned.1.call-done = bf16[512,1024]{1,0:T(8,128)(2,1)} async-done(((bf16[512,512]{1,0:T(8,128)(2,1)}), bf16[512,1024]{1,0:T(8,128)(2,1)}) %all-gather.5.cloned.1.call-update) | async-done | bytes 1048592 | tf_op jit(solution)/shard_map/all_gather | solution.py:51
  30.6 1.5 fusion.31
  32.1 6.3 %psum.14 = f32[512,1]{0,1:T(1,128)S(1)} all-reduce(f32[512,1]{0,1:T(1,128)S(1)} %bitcast.67), channel_id=1, replica_groups=mesh['replica'=1,'yz'=2,'x'=4] {'x'}, use_global_device_ids=true, to_apply=%region_1.0 | all-reduce | flops 512 | bytes 4096 | tf_op jit(solution)/shard_map/psum | solution.py:37
  38.4 7.1 %convolution_convert_fusion = bf16[512,2176]{0,1:T(8,128)(2,1)} fusion(bf16[1,4096,2176]{2,1,0:T(8,128)(2,1)} %param.14, s32[]{:T(128)} %bitcast.4, bf16[512,1024]{1,0:T(8,128)(2,1)} %all-gather.5.cloned.1.call-done, f32[1024]{0:T(1024)S(1)} %bitcast.70, f32[512]{0:T(512)S(1)} %bitcast.72), kind=kOutput, calls=%fused_computation.28 | convolution fusion | flops 2284912640 | bytes 7739904 | tf_op jit(solution)/shard_map/dot_general | solution.py:53
  45.6 0.0 reduce-scatter.5.cloned.1.call-update
  45.6 26.1 %reduce-scatter.5.cloned.1.call-done = bf16[512,544]{0,1:T(8,128)(2,1)} async-done(((bf16[512,2176]{0,1:T(8,128)(2,1)}), bf16[512,544]{0,1:T(8,128)(2,1)}) %reduce-scatter.5.cloned.1.call-update) | async-done | bytes 557072 | tf_op jit(solution)/shard_map/reduce_scatter | solution.py:54
  71.7 2.1 copy.14
  73.8 2.3 all-to-all-start
  76.1 0.0 all-gather.7.cloned.1.call-start
  76.1 0.0 copy-done.2
  76.2 0.2 iota_compare_fusion.1
  76.4 10.8 %all-to-all-done = bf16[8,64,544]{2,1,0:T(8,128)(2,1)S(1)} async-done(((bf16[8,64,544]{2,1,0:T(8,128)(2,1)}), bf16[8,64,544]{2,1,0:T(8,128)(2,1)S(1)}, u32[]{:S(2)}, u32[]{:S(2)}) %all-to-all-start) | async-done | bytes 557088 | tf_op jit(solution)/shard_map/all_to_all | solution.py:55
  87.2 0.4 copy.15
  87.5 0.5 all_to_all.31
  88.1 0.1 copy.18
  88.2 27.4 %fusion.2 = f32[64,32,2048]{2,1,0:T(8,128)} fusion(bf16[64,32,128]{2,1,0:T(8,128)(2,1)S(1)} %bitcast.65, bf16[1,64,2048,128]{3,2,1,0:T(8,128)(2,1)} %param.18, pred[64,2048]{1,0:T(8,128)(4,1)S(1)} %get-tuple-element.8, bf16[64,128]{1,0:T(8,128)(2,1)S(1)} %get-tuple-element.3), kind=kOutput, calls=%fused_computation.4 | convolution fusion | flops 1090519040 | bytes 51003392 | tf_op jit(solution)/shard_map/bhd,bsd->bhs/dot_general | solution.py:20
  115.6 19.6 %fusion.57 = (f32[64,32]{1,0:T(8,128)S(1)}, f32[64,32,2048]{2,1,0:T(8,128)}) fusion(f32[64,32,2048]{2,1,0:T(8,128)} %fusion.2, pred[64,2048]{1,0:T(8,128)(4,1)S(1)} %get-tuple-element.7), kind=kOutput, calls=%fused_computation.75 | output fusion | flops 25167872 | bytes 33693696 | tf_op jit(solution)/shard_map/sub | solution.py:23
  135.2 27.1 %fusion.43 = bf16[64,32,128]{2,1,0:T(8,128)(2,1)S(1)} fusion(bf16[1,64,2048,128]{3,2,1,0:T(8,128)(2,1)} %param.19, pred[64,2048]{1,0:T(8,128)(4,1)S(1)} %get-tuple-element.8, bf16[64,128]{1,0:T(8,128)(2,1)S(1)} %get-tuple-element.4, f32[64,32,2048]{2,1,0:T(8,128)} %get-tuple-element.10, f32[64,32]{1,0:T(8,128)S(1)} %get-tuple-element.9), kind=kOutput, calls=%fused_computation.53 | convolution fusion | flops 1099169792 | bytes 51011584 | tf_op jit(solution)/shard_map/bhs,bsd->bhd/dot_general | solution.py:24
  162.3 0.0 copy-start.1
  162.3 0.3 all_to_all.32
  162.6 0.2 copy.16
  162.8 11.5 %all_to_all.38 = bf16[64,8,512]{2,0,1:T(8,128)(2,1)} all-to-all(bf16[64,8,512]{2,0,1:T(8,128)(2,1)S(1)} %copy.16), channel_id=1, replica_groups=mesh['replica'=1,'yz'=2,'x'=4] {'yz','x'}, dimensions={1} | all-to-all | bytes 1048576 | tf_op jit(solution)/shard_map/all_to_all | solution.py:59
  174.3 0.0 all-gather.7.cloned.1.call-update
  174.3 0.0 reduce-scatter.7.cloned.1.call-start
  174.3 18.7 %all-gather.7.cloned.1.call-done = bf16[512,2048]{1,0:T(8,128)(2,1)} async-done(((bf16[512,512]{1,0:T(8,128)(2,1)}), bf16[512,2048]{1,0:T(8,128)(2,1)}) %all-gather.7.cloned.1.call-update) | async-done | bytes 2097168 | tf_op jit(solution)/shard_map/all_gather | solution.py:60
  193.1 6.7 %fusion.40 = bf16[512,1024]{1,0:T(8,128)(2,1)} fusion(bf16[512,2048]{1,0:T(8,128)(2,1)} %all-gather.7.cloned.1.call-done, bf16[1,2048,4096]{2,1,0:T(8,128)(2,1)} %param.15, s32[]{:T(128)} %bitcast.4), kind=kOutput, calls=%fused_computation.52 | convolution fusion | flops 2148007936 | bytes 7340544 | tf_op jit(solution)/shard_map/dot_general | solution.py:61
  199.7 0.0 reduce-scatter.7.cloned.1.call-update
  199.8 0.2 all-gather.9.cloned.1.call-start
  200.0 17.4 %reduce-scatter.7.cloned.1.call-done = bf16[512,512]{1,0:T(8,128)(2,1)} async-done(((bf16[512,1024]{1,0:T(8,128)(2,1)}), bf16[512,512]{1,0:T(8,128)(2,1)}) %reduce-scatter.7.cloned.1.call-update) | async-done | bytes 524304 | tf_op jit(solution)/shard_map/reduce_scatter | solution.py:42
  217.4 0.0 copy-done.1
  217.4 2.0 add_convert_fusion.1
  219.4 0.0 all-gather.9.cloned.1.call-update
  219.4 0.0 reduce-scatter.9.cloned.1.call-start
  219.5 24.2 %constant_dynamic-slice_fusion = bf16[1,1024,2,7168]{3,2,1,0:T(2,128)(2,1)} fusion(bf16[1,4096,2,7168]{3,2,1,0:T(2,128)(2,1)} %param.16, s32[]{:T(128)} %bitcast.4), kind=kLoop, calls=%fused_computation.69 | loop fusion | bytes 58720260 | tf_op jit(solution)/call_exported
  243.7 0.7 dynamic-slice_convert_fusion
  244.3 0.0 all-gather.9.cloned.1.call-done
  244.3 1.5 fusion.34
  245.8 6.3 %psum.15 = f32[512,1]{0,1:T(1,128)S(1)} all-reduce(f32[512,1]{0,1:T(1,128)S(1)} %bitcast.68), channel_id=1, replica_groups=mesh['replica'=1,'yz'=2,'x'=4] {'x'}, use_global_device_ids=true, to_apply=%region_7.8 | all-reduce | flops 512 | bytes 4096 | tf_op jit(solution)/shard_map/psum | solution.py:37
  252.1 25.4 %fusion.13 = bf16[512,2,7168]{2,0,1:T(8,128)(2,1)} fusion(bf16[1,1024,2,7168]{3,2,1,0:T(2,128)(2,1)} %constant_dynamic-slice_fusion, bf16[512,1024]{1,0:T(8,128)(2,1)} %all-gather.9.cloned.1.call-done, f32[1024]{0:T(1024)S(1)} %bitcast.69, f32[512]{0:T(512)S(1)} %bitcast.71), kind=kOutput, calls=%fused_computation.20 | convolution fusion | flops 15041822720 | bytes 45094912 | tf_op jit(solution)/shard_map/be,etf->btf/dot_general | solution.py:64
  277.5 0.0 reduce-scatter.9.cloned.1.call-update
  277.5 0.0 all-gather.11.cloned.1.call-start
  277.6 103.1 %reduce-scatter.9.cloned.1.call-done = bf16[512,2,1792]{2,0,1:T(8,128)(2,1)} async-done(((bf16[512,2,7168]{2,0,1:T(8,128)(2,1)}), bf16[512,2,1792]{2,0,1:T(8,128)(2,1)}) %reduce-scatter.9.cloned.1.call-update) | async-done | bytes 3670032 | tf_op jit(solution)/shard_map/reduce_scatter | solution.py:65
  380.7 4.4 fusion.30
  385.1 0.0 all-gather.11.cloned.1.call-update
  385.1 0.0 reduce-scatter.11.cloned.1.call-start
  385.1 49.8 %all-gather.11.cloned.1.call-done = bf16[512,7168]{1,0:T(8,128)(2,1)} async-done(((bf16[512,1792]{1,0:T(8,128)(2,1)}), bf16[512,7168]{1,0:T(8,128)(2,1)}) %all-gather.11.cloned.1.call-update) | async-done | bytes 7340048 | tf_op jit(solution)/shard_map/all_gather | solution.py:67
  434.9 14.5 %fusion.37 = bf16[512,1024]{1,0:T(8,128)(2,1)} fusion(bf16[512,7168]{1,0:T(8,128)(2,1)} %all-gather.11.cloned.1.call-done, bf16[1,7168,4096]{2,1,0:T(8,128)(2,1)} %param.17, s32[]{:T(128)} %bitcast.4), kind=kOutput, calls=%fused_computation.51 | convolution fusion | flops 7516717056 | bytes 23069184 | tf_op jit(solution)/shard_map/dot_general | solution.py:68
  449.4 0.0 reduce-scatter.11.cloned.1.call-update
  449.4 0.0 copy-start
  449.4 44.4 %broadcast_select_fusion = (bf16[1,64,2048,128]{3,2,1,0:T(8,128)(2,1)}, bf16[1,64,2048,128]{3,2,1,0:T(8,128)(2,1)}) fusion(bf16[1,64,2048,128]{3,2,1,0:T(8,128)(2,1)} %param.19, pred[64,2048]{1,0:T(8,128)(4,1)S(1)} %get-tuple-element.8, bf16[64,128]{1,0:T(8,128)(2,1)S(1)} %get-tuple-element.4, bf16[1,64,2048,128]{3,2,1,0:T(8,128)(2,1)} %param.18, ...), kind=kLoop, calls=%fused_computation.5 | loop fusion | flops 33554432 | bytes 134381568 | tf_op jit(solution)/shard_map/jit(_where)/select_n | solution.py:19
  493.8 0.0 reduce-scatter.11.cloned.1.call-done
  493.9 0.0 copy-done
  493.9 2.0 add_convert_fusion
  (4 shorter events, 0.1 us)
Async XLA Ops:
  7.2 69.0 %copy-start.2 = (s32[64]{0:T(128)S(1)}, s32[64]{0:T(128)}, u32[]{:S(2)}) copy-start(s32[64]{0:T(128)} %param.11) | copy-start | bytes 772
  7.2 23.4 %all-gather.5.cloned.1.call-start = ((), (), s32[]{:S(2)}) async-start(), calls=%async_computation.6 | async-start | bytes 1572864 | tf_op jit(solution)/shard_map/all_gather | solution.py:51
  7.9 63.8 %reduce-scatter.5.cloned.1.call-start = ((), (), s32[]{:S(2)}) async-start(), calls=%async_computation.7 | async-start | bytes 2785280 | tf_op jit(solution)/shard_map/reduce_scatter | solution.py:54
  73.8 13.3 %all-to-all-start = ((bf16[8,64,544]{2,1,0:T(8,128)(2,1)}), bf16[8,64,544]{2,1,0:T(8,128)(2,1)S(1)}, u32[]{:S(2)}, u32[]{:S(2)}) async-start(bf16[8,64,544]{2,1,0:T(8,128)(2,1)} %bitcast.6), calls=%async_computation.1 | async-start | bytes 1310720 | tf_op jit(solution)/shard_map/all_to_all | solution.py:55
  76.1 117.0 %all-gather.7.cloned.1.call-start = ((), (), s32[]{:S(2)}) async-start(), calls=%async_computation.8 | async-start | bytes 2621440 | tf_op jit(solution)/shard_map/all_gather | solution.py:60
  162.3 55.1 %copy-start.1 = (bf16[512,512]{1,0:T(8,128)(2,1)S(1)}, bf16[512,512]{1,0:T(8,128)(2,1)}, u32[]{:S(2)}) copy-start(bf16[512,512]{1,0:T(8,128)(2,1)} %param.10) | copy-start | bytes 1572868
  174.3 43.1 %reduce-scatter.7.cloned.1.call-start = ((), (), s32[]{:S(2)}) async-start(), calls=%async_computation.9 | async-start | bytes 1572864 | tf_op jit(solution)/shard_map/reduce_scatter | solution.py:42
  199.8 44.6 %all-gather.9.cloned.1.call-start = ((), (), s32[]{:S(2)}) async-start(), calls=%async_computation.10 | async-start | bytes 1572864 | tf_op jit(solution)/shard_map/all_gather | solution.py:62
  219.4 161.2 %reduce-scatter.9.cloned.1.call-start = ((), (), s32[]{:S(2)}) async-start(), calls=%async_computation.11 | async-start | bytes 18350080 | tf_op jit(solution)/shard_map/reduce_scatter | solution.py:65
  277.5 157.4 %all-gather.11.cloned.1.call-start = ((), (), s32[]{:S(2)}) async-start(), calls=%async_computation.12 | async-start | bytes 9175040 | tf_op jit(solution)/shard_map/all_gather | solution.py:67
  385.1 108.8 %reduce-scatter.11.cloned.1.call-start = ((), (), s32[]{:S(2)}) async-start(), calls=%async_computation.13 | async-start | bytes 1572864 | tf_op jit(solution)/shard_map/reduce_scatter | solution.py:42
  449.4 44.4 %copy-start = (bf16[512,512]{1,0:T(8,128)(2,1)S(1)}, bf16[512,512]{1,0:T(8,128)(2,1)}, u32[]{:S(2)}) copy-start(bf16[512,512]{1,0:T(8,128)(2,1)} %add_convert_fusion.1) | copy-start | bytes 1572868
Sparse Core Ops, SparseCore 0:
  9.5 21.0 all-gather.4
  45.7 25.9 reduce-scatter.4
  174.4 18.6 all-gather.6
  199.9 17.5 reduce-scatter.6
  219.5 18.2 all-gather.8
  277.7 102.9 reduce-scatter.8
  385.2 49.6 all-gather.10
  449.6 17.5 reduce-scatter.10
where the time goes:
time: 503 us
  waiting for transfers between devices  246 us (49%)
  matrix products  108 us (21%)
  other arithmetic  76.9 us (15%)
  local copies, waits for them, and re-layouts  30.3 us (6%)
  blocking collectives  24.1 us (5%)
  between operations  14.9 us (3%)
    reduce_scatter x1, waiting for transfers between devices, local_step(): gu_cols = lax.psum_scatter(gu_part, 'x', scatter_dimension=2, tiled=True)  103 us
    all_gather x1, waiting for transfers between devices, local_step(): mlp_slab = lax.all_gather(mlp_cols, 'x', axis=1, tiled=True)  49.8 us
    select_n x1, other arithmetic, attend(): v_upd = jnp.where(at_slot, v_new[:, None, :], v_layer)  44.4 us
    dot_general x1, matrix products, attend(): jnp.einsum('bhd,bsd->bhs', queries, k_upd, preferred_element_type=jnp.flo...  27.4 us
    dot_general x1, matrix products, attend(): jnp.einsum('bhs,bsd->bhd', probs_bf, v_upd, preferred_element_type=jnp.fl...  27.1 us
    another operation x3, local copies, waits for them, and re-layouts  26.6 us
    reduce_scatter x1, waiting for transfers between devices, local_step(): z_cols = lax.psum_scatter(partial_z, 'x', scatter_dimension=1, tiled=True)  26.1 us
    dot_general x1, matrix products, local_step(): jnp.einsum('be,etf->btf', normed, w_gate_up[layer_idx], preferred_element...  25.4 us
  transfers between devices with their start and end apart: 9, of which 7 were waited for; matrix products, arithmetic and copies ran while one was open for 14% of the time, Pallas kernels for 0%

commit v1 on v0

v1 whole, which is shorter than its diff:
```python
import functools

import jax
import jax.numpy as jnp
from jax import lax
from jax.experimental import pallas as pl
from jax.experimental.pallas import tpu as pltpu
from jax.sharding import PartitionSpec as P

NORM_EPS = 1e-5
MESH = pl.DeviceIdType.MESH
MIB = 1 << 20
VMEM = pltpu.VMEM
DMA = pltpu.SemaphoreType.DMA


def place():
    yz = lax.axis_index('yz')
    x = lax.axis_index('x')
    return yz, x // 2, x % 2


def device(yz, chip, core):
    return {'yz': yz, 'x': 2 * chip + core}


def remote(src, dst, send, recv, target):
    return pltpu.make_async_remote_copy(src_ref=src, dst_ref=dst, send_sem=send, recv_sem=recv,
                                        device_id=target, device_id_type=MESH)


def greet(peers):
    barrier = pltpu.get_barrier_semaphore()
    for peer in peers:
        pl.semaphore_signal(barrier, inc=1, device_id=peer, device_id_type=MESH)
    pl.semaphore_wait(barrier, len(peers))


def lanes(start, size, unit=128):
    return pl.ds(pl.multiple_of(start, unit), size)


def dot(a, b):
    return jnp.dot(a, b, preferred_element_type=jnp.float32)


def qkv_kernel(h_ref, gain_ref, w_ref, z_ref, hx_ref, wbuf, ubuf, zbuf, w_sem, send, recv, zsend, zrecv):
    yz, chip, core = place()
    cols = h_ref.shape[-1]
    width = z_ref.shape[-1]
    parts = ((0, 512), (512, width - 512))
    step = w_ref.shape[1] - width
    model = hx_ref.shape[-1]
    loads = []
    for n, (off, size) in enumerate(parts):
        loads.append(pltpu.make_async_copy(w_ref.at[:, lanes(core * step + off, size)],
                                           wbuf.at[:, pl.ds(off, size)], w_sem.at[n]))
        loads[-1].start()
    ynbr, xnbr = device(1 - yz, chip, core), device(yz, 1 - chip, core)
    diag, partner = device(1 - yz, 1 - chip, core), device(yz, chip, 1 - core)
    far = device(1 - yz, chip, 1 - core)
    greet((ynbr, xnbr, diag, partner, far))

    def block(y, ch, co):
        return hx_ref.at[:, :, lanes((2 * (2 * ch + co) + y) * cols, cols, 512)]

    mine = block(yz, chip, core)
    copies = []
    for k, (src, target) in enumerate(((1 - chip, diag), (chip, ynbr), (1 - chip, xnbr), (chip, partner))):
        copies.append(remote(h_ref.at[:, src], mine, send.at[k], recv.at[k], target))
        copies[-1].start()
    hx_ref[:, :, lanes((2 * (2 * chip + core) + yz) * cols, cols, 512)] = h_ref[:, chip]
    arrivals = ((1, block(1 - yz, chip, core)), (2, block(yz, 1 - chip, core)), (0, block(1 - yz, 1 - chip, core)))
    for k, (which, ref) in enumerate(arrivals):
        copies[which].wait_recv()
        copies.append(remote(ref, ref, send.at[4 + k], recv.at[4 + k], partner))
        copies[-1].start()
    for k in (3, 4, 5, 6):
        copies[k].wait_recv()

    gain = gain_ref[...].astype(jnp.float32)
    chunk = 32
    for half in range(2):
        @pl.loop(0, 128 // chunk)
        def _(r):
            hid = hx_ref[half, lanes(r * chunk, chunk, chunk), :].astype(jnp.float32)
            inv = lax.rsqrt(jnp.sum(hid * hid, axis=1, keepdims=True) / model + NORM_EPS)
            ubuf[lanes(half * 128 + r * chunk, chunk, chunk), :] = (hid * inv * gain).astype(jnp.bfloat16)

    slot = 2 * yz + core
    zcopies = []
    for n, (off, size) in enumerate(parts):
        loads[n].wait()
        z = dot(ubuf[...], wbuf[:, off:off + size]).astype(jnp.bfloat16)
        zbuf[:, :, off:off + size] = z.reshape(4, 64, size)
        for k, (y, co, target) in enumerate(((1 - yz, core, ynbr), (1 - yz, 1 - core, far), (yz, 1 - core, partner))):
            zcopies.append(remote(zbuf.at[2 * y + co, :, pl.ds(off, size)], z_ref.at[slot, :, pl.ds(off, size)],
                                  zsend.at[n, k], zrecv.at[n, k], target))
            zcopies[-1].start()
    z_ref[slot] = zbuf[slot]
    for copy in copies:
        copy.wait_send()
    for copy in zcopies:
        copy.wait()


def project_qkv(h, gain, w_qkv):
    model, half = w_qkv.shape
    width = (half // 128 + 1) // 2 * 128
    h4 = h.reshape(2, 2, 128, h.shape[1])
    return pl.pallas_call(
        qkv_kernel,
        out_shape=(jax.ShapeDtypeStruct((4, 64, width), jnp.bfloat16),
                   jax.ShapeDtypeStruct((2, 128, model), jnp.bfloat16)),
        in_specs=[pl.BlockSpec(memory_space=VMEM), pl.BlockSpec(memory_space=VMEM), pl.BlockSpec(memory_space=pl.ANY)],
        out_specs=(pl.BlockSpec(memory_space=VMEM), pl.BlockSpec(memory_space=VMEM)),
        scratch_shapes=[VMEM((model, width), jnp.bfloat16), VMEM((256, model), jnp.bfloat16),
                        VMEM((4, 64, width), jnp.bfloat16), DMA((2,)), DMA((7,)), DMA((7,)), DMA((2, 3)), DMA((2, 3))],
        compiler_params=pltpu.CompilerParams(collective_id=0, has_side_effects=True, vmem_limit_bytes=40 * MIB),
        name='qkv',
    )(h4, gain, w_qkv)


def attention_kernel(lens_ref, z_ref, k_ref, v_ref, o_ref, ko_ref, vo_ref, qs, kn, vn, os, kbuf, vbuf, isem, osem, *,
                     heads, slots, ahead):
    seqs, length, dim = k_ref.shape
    tiles = (heads + 2) // 2
    split = tiles // 2

    def tile(t):
        y, local = t // tiles, t % tiles
        co = 1 if local >= split else 0
        first = (local - split * co) * dim
        return z_ref[2 * y + co, :, first:first + dim].astype(jnp.float32)

    def fetch(b):
        s = lax.rem(b, slots)
        return (pltpu.make_async_copy(k_ref.at[b], kbuf.at[s], isem.at[0, s]),
                pltpu.make_async_copy(v_ref.at[b], vbuf.at[s], isem.at[1, s]))

    def flush(b):
        s = lax.rem(b, slots)
        return (pltpu.make_async_copy(kbuf.at[s], ko_ref.at[b], osem.at[0, s]),
                pltpu.make_async_copy(vbuf.at[s], vo_ref.at[b], osem.at[1, s]))

    for b in range(ahead):
        for copy in fetch(jnp.int32(b)):
            copy.start()
    for t in range(heads):
        qs[pl.ds(t, seqs, stride=heads), :] = tile(t)
    kn[...] = tile(heads)
    vn[...] = tile(heads + 1)

    @pl.loop(0, seqs)
    def _(b):
        nxt = b + ahead

        @pl.when(nxt < seqs)
        def _():
            @pl.when(nxt >= slots)
            def _():
                for copy in flush(nxt - slots):
                    copy.wait()
            for copy in fetch(nxt):
                copy.start()

        s = lax.rem(b, slots)
        for copy in fetch(b):
            copy.wait()
        last = lens_ref[b]
        base = pl.multiple_of(last // 16 * 16, 16)
        row = lax.broadcasted_iota(jnp.int32, (16, dim), 0) == last - base
        for buf, new in ((kbuf, kn), (vbuf, vn)):
            old = buf[s, pl.ds(base, 16), :].astype(jnp.float32)
            buf[s, pl.ds(base, 16), :] = jnp.where(row, new[pl.ds(b, 1), :], old).astype(jnp.bfloat16)
        for copy in flush(b):
            copy.start()
        q = qs[lanes(b * heads, heads, heads), :].astype(jnp.bfloat16)
        scores = lax.dot_general(q, kbuf[s], (((1,), (1,)), ((), ())), preferred_element_type=jnp.float32) * dim ** -0.5
        seen = lax.broadcasted_iota(jnp.int32, (heads, length), 1) <= last
        scores = jnp.where(seen, scores, -1e30)
        probs = jnp.exp(scores - jnp.max(scores, axis=1, keepdims=True))
        probs = probs * (1.0 / jnp.sum(probs, axis=1, keepdims=True))
        os[lanes(b * heads, heads, heads), :] = dot(probs.astype(jnp.bfloat16), vbuf[s])

    for t in range(heads):
        o_ref[:, t * dim:(t + 1) * dim] = os[pl.ds(t, seqs, stride=heads), :].astype(jnp.bfloat16)

    @pl.loop(seqs - slots, seqs)
    def _(b):
        for copy in flush(b):
            copy.wait()


def attend(lens, z, k_cache, v_cache):
    seqs, length, dim = k_cache.shape
    heads = 32
    slots, ahead = 12, 6
    anywhere = pl.BlockSpec(memory_space=pl.ANY)
    vmem = pl.BlockSpec(memory_space=VMEM)
    return pl.pallas_call(
        functools.partial(attention_kernel, heads=heads, slots=slots, ahead=ahead),
        out_shape=(jax.ShapeDtypeStruct((seqs, heads * dim), jnp.bfloat16),
                   jax.ShapeDtypeStruct(k_cache.shape, k_cache.dtype),
                   jax.ShapeDtypeStruct(v_cache.shape, v_cache.dtype)),
        in_specs=[pl.BlockSpec(memory_space=pltpu.SMEM), vmem, anywhere, anywhere],
        out_specs=(vmem, anywhere, anywhere),
        scratch_shapes=[VMEM((seqs * heads, dim), jnp.float32), VMEM((seqs, dim), jnp.float32),
                        VMEM((seqs, dim), jnp.float32), VMEM((seqs * heads, dim), jnp.float32),
                        VMEM((slots, length, dim), jnp.bfloat16), VMEM((slots, length, dim), jnp.bfloat16),
                        DMA((2, slots)), DMA((2, slots))],
        compiler_params=pltpu.CompilerParams(vmem_limit_bytes=40 * MIB),
        name='attention',
    )(lens, z, k_cache, v_cache)


def mlp_kernel(o_ref, hx_ref, gain_ref, spread_ref, wo_ref, gu_ref, wd_ref, out_ref,
               og, hres, wo, ys, yr, h1, ubuf, ue, gub, mbuf, wd, ps, pr, acc, fs, fr, xs,
               s_wo, s_h, s_gu, s_wd, send, recv, ysend, yrecv, hsend, hrecv, psend, precv, fsend, frecv, xsend, xrecv):
    yz, chip, core = place()
    half = wo_ref.shape[0]
    model = wo_ref.shape[1]
    inner = gu_ref.shape[2] // 2
    ynbr, xnbr, partner = device(1 - yz, chip, core), device(yz, 1 - chip, core), device(yz, chip, 1 - core)

    wo_copies = [pltpu.make_async_copy(wo_ref.at[:, lanes(core * half + n * 512, 512, 512)], wo.at[n], s_wo.at[n])
                 for n in range(4)]
    h_copy = pltpu.make_async_copy(hx_ref.at[:, :, lanes(core * half, half, 512)], hres, s_h.at[0])

    def gu_copies(n):
        s = lax.rem(n, 2)
        return [pltpu.make_async_copy(gu_ref.at[pl.ds(r * 1024, 1024), :, lanes(core * inner + n * 512, 512, 512)],
                                      gub.at[s, pl.ds(r * 1024, 1024)], s_gu.at[s, r]) for r in range(4)]

    def column(t):
        k = t // 2
        y = jnp.where(k < 2, 1 - yz, yz)
        ch = jnp.where(k % 2 == 0, 1 - chip, chip)
        co = jnp.where(t % 2 == 0, 1 - core, core)
        return 2 * (2 * ch + co) + y

    def wd_copies(t):
        s = lax.rem(t, 3)
        rows = inner // 2
        return [pltpu.make_async_copy(wd_ref.at[lanes(core * inner + r * rows, rows, rows), lanes(column(t) * 512, 512, 512)],
                                      wd.at[s, pl.ds(r * rows, rows)], s_wd.at[s, r]) for r in range(2)]

    for copy in wo_copies:
        copy.start()
    h_copy.start()
    greet((ynbr, xnbr, partner))

    slot = 2 * yz + core
    to_y = remote(o_ref.at[:, lanes((1 - yz) * half, half, 512)], og.at[slot], send.at[0], recv.at[0], ynbr)
    to_y.start()
    to_p = remote(o_ref.at[:, lanes(yz * half, half, 512)], og.at[slot], send.at[1], recv.at[1], partner)
    to_p.start()
    og[slot] = o_ref[:, lanes(yz * half, half, 512)]
    for n in range(2):
        for copy in gu_copies(jnp.int32(n)):
            copy.start()
    for t in range(3):
        for copy in wd_copies(jnp.int32(t)):
            copy.start()
    to_y.wait_recv()
    theirs = og.at[2 * (1 - yz) + core]
    onward = remote(theirs, theirs, send.at[2], recv.at[2], partner)
    onward.start()
    to_p.wait_recv()
    onward.wait_recv()

    def y_copy(n):
        return remote(ys.at[n], yr.at[n], ysend.at[n], yrecv.at[n], ynbr)

    for copy in wo_copies:
        copy.wait()

    @pl.loop(0, 4)
    def _(n):
        ys[n] = dot(og[...].reshape(256, half), wo[n]).astype(jnp.bfloat16)
        y_copy(n).start()

    h_copy.wait()

    def h_send(n):
        return remote(h1.at[4 * core + n], h1.at[4 * core + n], hsend.at[n], hrecv.at[n], partner)

    @pl.loop(0, 4)
    def _(n):
        y_copy(n).wait_recv()
        total = ys[n].astype(jnp.float32) + yr[n].astype(jnp.float32)
        res = hres[:, :, lanes(n * 512, 512, 512)].reshape(256, 512).astype(jnp.float32)
        h1[4 * core + n] = (res + total).astype(jnp.bfloat16)
        h_send(n).start()

    @pl.loop(0, 4)
    def _(n):
        h_send(n).wait_recv()

    gain = gain_ref[...].astype(jnp.float32)

    @pl.loop(0, 8)
    def _(r):
        rows = lanes(r * 32, 32, 32)
        power = jnp.zeros((32, 1), jnp.float32)
        for n in range(8):
            hid = h1[n, rows, :].astype(jnp.float32)
            power += jnp.sum(hid * hid, axis=1, keepdims=True)
        inv = lax.rsqrt(power / model + NORM_EPS)
        for n in range(8):
            hid = h1[n, rows, :].astype(jnp.float32)
            ubuf[rows, n * 512:(n + 1) * 512] = (hid * inv * gain[:, n * 512:(n + 1) * 512]).astype(jnp.bfloat16)

    spread = spread_ref[...]

    @pl.loop(0, model // 512)
    def _(t):
        for q in range(4):
            wide = dot(ubuf[:, lanes(t * 512 + q * 128, 128)], spread).astype(jnp.bfloat16)
            ue[:256, lanes(t * 1024 + q * 256, 256, 256)] = wide[:, :256]
            ue[256:, lanes(t * 1024 + q * 256, 256, 256)] = wide[:, 256:]

    @pl.loop(0, inner // 512)
    def _(n):
        s = lax.rem(n, 2)
        for copy in gu_copies(n):
            copy.wait()
        both = dot(ue[...], gub.at[s].reshape(2 * model, 512)[...])

        @pl.when(n + 2 < inner // 512)
        def _():
            for copy in gu_copies(n + 2):
                copy.start()

        gate = both[:256].astype(jnp.bfloat16).astype(jnp.float32)
        up = both[256:].astype(jnp.bfloat16).astype(jnp.float32)
        mbuf[:, lanes(n * 512, 512, 512)] = (gate * jax.nn.sigmoid(gate) * up).astype(jnp.bfloat16)

    def p_copy(k):
        return remote(ps.at[k], pr.at[k], psend.at[k], precv.at[k], partner)

    def f_copy(k):
        return remote(fs.at[k], fr.at[k], fsend.at[k], frecv.at[k], ynbr)

    x_copy = remote(xs, out_ref.at[:, chip], xsend.at[0], xrecv.at[0], xnbr)

    @pl.loop(0, 4)
    def _(k):
        for side in range(2):
            t = 2 * k + side
            s = lax.rem(t, 3)
            for copy in wd_copies(t):
                copy.wait()
            part = dot(mbuf[...], wd[s])

            @pl.when(t + 3 < 8)
            def _():
                for copy in wd_copies(t + 3):
                    copy.start()

            if side == 0:
                ps[k] = part.astype(jnp.bfloat16)
                p_copy(k).start()
            else:
                acc[...] = part
        p_copy(k).wait_recv()
        acc[...] += pr[k].astype(jnp.float32)

        @pl.when(k < 2)
        def _():
            fs[k] = acc[...].astype(jnp.bfloat16)
            f_copy(k).start()

        @pl.when(k >= 2)
        def _():
            f_copy(k - 2).wait_recv()
            total = acc[...] + fr[k - 2].astype(jnp.float32)
            final = (h1[column(2 * k + 1)].astype(jnp.float32) + total).astype(jnp.bfloat16).reshape(2, 128, 512)

            @pl.when(k == 2)
            def _():
                xs[...] = final
                x_copy.start()

            @pl.when(k == 3)
            def _():
                out_ref[:, chip] = final

    x_copy.wait()
    for copy in (to_y, to_p, onward):
        copy.wait_send()

    @pl.loop(0, 4)
    def _(n):
        y_copy(n).wait_send()
        h_send(n).wait_send()
        p_copy(n).wait_send()

    @pl.loop(0, 2)
    def _(n):
        f_copy(n).wait_send()


def mlp(o, hx, gain, w_out, w_gate_up, w_down):
    half, model = w_out.shape
    inner = w_gate_up.shape[2] // 2
    anywhere = pl.BlockSpec(memory_space=pl.ANY)
    vmem = pl.BlockSpec(memory_space=VMEM)
    bf16 = jnp.bfloat16
    column = jnp.arange(512)[None, :]
    spread = (column % 256 == 2 * jnp.arange(128)[:, None] + column // 256).astype(bf16)
    out = pl.pallas_call(
        mlp_kernel,
        out_shape=jax.ShapeDtypeStruct((2, 2, 128, 512), bf16),
        in_specs=[vmem, anywhere, vmem, vmem, anywhere, anywhere, anywhere],
        out_specs=vmem,
        scratch_shapes=[
            VMEM((4, 64, half), bf16), VMEM((2, 128, half), bf16), VMEM((4, half, 512), bf16),
            VMEM((4, 256, 512), bf16), VMEM((4, 256, 512), bf16), VMEM((8, 256, 512), bf16),
            VMEM((256, model), bf16), VMEM((512, 2 * model), bf16), VMEM((2, model, 2, 512), bf16),
            VMEM((256, inner), bf16), VMEM((3, inner, 512), bf16),
            VMEM((4, 256, 512), bf16), VMEM((4, 256, 512), bf16), VMEM((256, 512), jnp.float32),
            VMEM((2, 256, 512), bf16), VMEM((2, 256, 512), bf16), VMEM((2, 128, 512), bf16),
            DMA((4,)), DMA((1,)), DMA((2, 4)), DMA((3, 2)),
            DMA((3,)), DMA((3,)), DMA((4,)), DMA((4,)), DMA((4,)), DMA((4,)), DMA((4,)), DMA((4,)),
            DMA((2,)), DMA((2,)), DMA((1,)), DMA((1,)),
        ],
        compiler_params=pltpu.CompilerParams(collective_id=1, has_side_effects=True, vmem_limit_bytes=67043328),
        name='mlp',
    )(o, hx, gain, spread, w_out, w_gate_up, w_down)
    return out.reshape(512, 512)


def solution(mesh):
    batch_axes = ('replica', 'yz', 'x')
    hidden_spec = P('replica', ('x', 'yz'))
    cache_spec = P(None, batch_axes, None, None)

    def local_step(hidden, seq_lens, attn_gain, mlp_gain, w_qkv, w_out, w_gate_up, w_down, k_cache, v_cache):
        k_layers = []
        v_layers = []
        for layer in range(w_qkv.shape[0]):
            z, hx = project_qkv(hidden, attn_gain[layer:layer + 1], w_qkv[layer])
            o, k_upd, v_upd = attend(seq_lens, z, k_cache[layer], v_cache[layer])
            k_layers.append(k_upd)
            v_layers.append(v_upd)
            hidden = mlp(o, hx, mlp_gain[layer:layer + 1], w_out[layer], w_gate_up[layer], w_down[layer])
        return hidden, jnp.stack(k_layers), jnp.stack(v_layers)

    return jax.shard_map(
        local_step,
        mesh=mesh,
        in_specs=(hidden_spec, P(batch_axes), P(None, None), P(None, None), P(None, None, 'yz'), P(None, 'yz', None),
                  P(None, None, None, 'yz'), P(None, 'yz', None), cache_spec, cache_spec),
        out_specs=(hidden_spec, cache_spec, cache_spec),
        check_vma=False)
```

time: 503 us -> 175 us (0.35)
  waiting for transfers between devices: 246 us -> 0 us
  Pallas kernels: 0 us -> 168 us
  matrix products: 108 us -> 0 us
  other arithmetic: 76.9 us -> 0.76 us
  local copies, waits for them, and re-layouts: 30.3 us -> 5.09 us
  blocking collectives: 24.1 us -> 0 us
  between operations: 14.9 us -> 0.7 us
    pallas_call x0 -> x3, Pallas kernels: none -> 168 us  [the longest x1 92.2 us: mlp(): pl.pallas_call(mlp_kernel, out_shape=jax.ShapeDtypeStruct((2, 2, 128, 512...]
    reduce_scatter x4 -> x0, waiting for transfers between devices: 147 us -> none  [the longest x1 103 us: local_step(): gu_cols = lax.psum_scatter(gu_part, 'x', scatter_dimension=2, tiled=True)]
    dot_general x6 -> x0, matrix products: 108 us -> none  [the longest x1 27.4 us: attend(): jnp.einsum('bhd,bsd->bhs', queries, k_upd, preferred_element_type=jnp.flo...]
    all_gather x4 -> x0, waiting for transfers between devices: 87.4 us -> none  [the longest x1 49.8 us: local_step(): mlp_slab = lax.all_gather(mlp_cols, 'x', axis=1, tiled=True)]
    select_n x1, other arithmetic: 44.4 us -> 0.01 us  [mlp(): column // 256]
    another operation x3 -> x0, local copies, waits for them, and re-layouts: 26.6 us -> none
    sub x1 -> x0, other arithmetic: 19.6 us -> none  [attend(): probs_bf = jax.nn.softmax(scores, axis=-1).astype(jnp.bfloat16)]
    psum x2 -> x0, blocking collectives: 12.6 us -> none  [norm_part(): sq_power = lax.psum(jnp.sum(hid_f * hid_f, axis=1, keepdims=True), 'x')]
  transfers between devices with their start and end apart: 9 -> 0, of which waited for: 7 -> 0; matrix products, arithmetic and copies ran while one was open for 14% -> 0% of each run, Pallas kernels for 0% -> 0%
where the time goes in v1:
time: 175 us
  Pallas kernels  168 us (96%)
  local copies, waits for them, and re-layouts  5.09 us (3%)
    pallas_call x1, Pallas kernels, mlp(): pl.pallas_call(mlp_kernel, out_shape=jax.ShapeDtypeStruct((2, 2, 128, 512...  92.2 us
    pallas_call x1, Pallas kernels, attend(): pl.pallas_call(functools.partial(attention_kernel, heads=heads, slots=slo...  46.7 us
    pallas_call x1, Pallas kernels, project_qkv(): pl.pallas_call(qkv_kernel, out_shape=(jax.ShapeDtypeStruct((4, 64, width)...  29.6 us
    unnamed x11, local copies, waits for them, and re-layouts  5.09 us

profile of v1, /device:TPU:0, one launch (start us, length us, event | category | flops | bytes accessed | tf_op | source)
XLA Modules:
  0.0 175.0 jit_solution(16459444298191669283)
XLA Ops:
  0.6 0.0 copy-start.2
  0.6 1.0 copy-done.2
  1.7 0.0 copy-start.3
  1.7 0.7 copy-done.3
  2.4 29.6 %qkv.1 = (bf16[4,64,1152]{2,1,0:T(8,128)(2,1)S(1)}, bf16[2,128,4096]{2,1,0:T(8,128)(2,1)S(1)}) custom-call(bf16[2,2,128,512]{3,2,1,0:T(8,128)(2,1)S(1)} %bitcast.10, bf16[1,4096]{1,0:T(2,128)(2,1)S(1)} %copy-done.3, bf16[4096,2176]{1,0:T(8,128)(2,1)} %bitcast.14), custom_call_target="tpu_custom_call" | custom-call | tf_op jit(solution)/shard_map/qkv/pallas_call | solution.py:111
  32.0 0.0 copy-start
  32.0 0.0 copy-start.4
  32.0 0.7 copy-done.4
  32.7 46.7 %attention.1 = (bf16[64,4096]{1,0:T(8,128)(2,1)S(1)}, bf16[64,2048,128]{2,1,0:T(8,128)(2,1)}, bf16[64,2048,128]{2,1,0:T(8,128)(2,1)}) custom-call(s32[64]{0:T(128)S(1)} %copy-done.4, bf16[4,64,1152]{2,1,0:T(8,128)(2,1)S(1)} %get-tuple-element.8.z_ref, bf16[64,2048,128]{2,1,0:T(8,128)(2,1)} %bitcast.12, bf16[64,2048,128]{2,1,0:T(8,128)(2,1)} %bitcast.13), custom_call_target="tpu_custom_call" | custom-call | tf_op jit(solution)/shard_map/attention/pallas_call | solution.py:201
  79.4 0.0 copy-done
  79.4 0.0 copy-start.1
  79.4 0.8 copy-done.1
  80.2 0.8 fusion.spread_ref
  81.0 92.2 %mlp.1 = bf16[2,2,128,512]{3,2,1,0:T(8,128)(2,1)} custom-call(bf16[64,4096]{1,0:T(8,128)(2,1)} %copy-done.1, bf16[2,128,4096]{2,1,0:T(8,128)(2,1)} %copy-done, bf16[1,4096]{1,0:T(2,128)(2,1)} %gain_ref.3, bf16[128,512]{1,0:T(8,128)(2,1)} %fusion.spread_ref, bf16[2048,4096]{1,0:T(8,128)(2,1)} %bitcast.15, bf16[4096,2,7168]{2,1,0:T(2,128)(2,1)} %bitcast.5.gu_ref, ...), custom_call_target="tpu_custom_call" | custom-call | tf_op jit(solution)/shard_map/mlp/pallas_call | solution.py:412
  173.2 1.9 %copy.14 = bf16[512,512]{1,0:T(8,128)(2,1)} copy(bf16[512,512]{1,0:T(8,128)(2,1)} %bitcast.16) | data formatting | bytes 1048576
  (2 shorter events, 0.0 us)
Async XLA Ops:
  0.6 1.0 copy-start.2
  1.7 0.7 copy-start.3
  32.0 47.4 %copy-start = (bf16[2,128,4096]{2,1,0:T(8,128)(2,1)}, bf16[2,128,4096]{2,1,0:T(8,128)(2,1)S(1)}, u32[]{:S(2)}) copy-start(bf16[2,128,4096]{2,1,0:T(8,128)(2,1)S(1)} %get-tuple-element.10.hx_ref) | copy-start | bytes 6291460
  32.0 0.7 copy-start.4
  79.4 0.8 copy-start.1

commit v2 on v1

v2 whole, which is shorter than its diff:
```python
import functools

import jax
import jax.numpy as jnp
from jax import lax
from jax.experimental import pallas as pl
from jax.experimental.pallas import tpu as pltpu
from jax.sharding import PartitionSpec as P

NORM_EPS = 1e-5
MESH = pl.DeviceIdType.MESH
MIB = 1 << 20
GROUP, DEPTH = 4, 4
VMEM = pltpu.VMEM
DMA = pltpu.SemaphoreType.DMA


def place():
    yz = lax.axis_index('yz')
    x = lax.axis_index('x')
    return yz, x // 2, x % 2


def device(yz, chip, core):
    return {'yz': yz, 'x': 2 * chip + core}


def remote(src, dst, send, recv, target):
    return pltpu.make_async_remote_copy(src_ref=src, dst_ref=dst, send_sem=send, recv_sem=recv,
                                        device_id=target, device_id_type=MESH)


def greet(peers):
    barrier = pltpu.get_barrier_semaphore()
    for peer in peers:
        pl.semaphore_signal(barrier, inc=1, device_id=peer, device_id_type=MESH)
    pl.semaphore_wait(barrier, len(peers))


def lanes(start, size, unit=128):
    return pl.ds(pl.multiple_of(start, unit), size)


def slot_columns(yz, core):
    return core * 2048 + yz * 1024


def dot(a, b):
    return jnp.dot(a, b, preferred_element_type=jnp.float32)


def qkv_kernel(h_ref, gain_ref, w_ref, z_ref, hres_ref, hx_ref, wbuf, ubuf, zbuf, w_sem, send, recv, zsend, zrecv):
    yz, chip, core = place()
    cols = h_ref.shape[-1]
    width = z_ref.shape[-1]
    parts = ((0, 512), (512, width - 512))
    step = w_ref.shape[1] - width
    model = hx_ref.shape[-1]
    loads = []
    for n, (off, size) in enumerate(parts):
        loads.append(pltpu.make_async_copy(w_ref.at[:, lanes(core * step + off, size)],
                                           wbuf.at[:, pl.ds(off, size)], w_sem.at[n]))
        loads[-1].start()
    ynbr, xnbr = device(1 - yz, chip, core), device(yz, 1 - chip, core)
    diag, partner = device(1 - yz, 1 - chip, core), device(yz, chip, 1 - core)
    far = device(1 - yz, chip, 1 - core)
    greet((ynbr, xnbr, diag, partner, far))

    def block(y, ch, co):
        return hx_ref.at[:, :, lanes((2 * (2 * ch + co) + y) * cols, cols, 512)]

    mine = block(yz, chip, core)
    copies = []
    for k, (src, target) in enumerate(((1 - chip, diag), (chip, ynbr), (1 - chip, xnbr), (chip, partner))):
        copies.append(remote(h_ref.at[:, src], mine, send.at[k], recv.at[k], target))
        copies[-1].start()
    hx_ref[:, :, lanes((2 * (2 * chip + core) + yz) * cols, cols, 512)] = h_ref[:, chip]
    arrivals = ((1, block(1 - yz, chip, core)), (2, block(yz, 1 - chip, core)), (0, block(1 - yz, 1 - chip, core)))
    for k, (which, ref) in enumerate(arrivals):
        copies[which].wait_recv()
        copies.append(remote(ref, ref, send.at[4 + k], recv.at[4 + k], partner))
        copies[-1].start()
    for k in (3, 4, 5, 6):
        copies[k].wait_recv()

    gain = gain_ref[...].astype(jnp.float32)
    chunk = 32
    for half in range(2):
        @pl.loop(0, 128 // chunk)
        def _(r):
            hid = hx_ref[half, lanes(r * chunk, chunk, chunk), :].astype(jnp.float32)
            inv = lax.rsqrt(jnp.sum(hid * hid, axis=1, keepdims=True) / model + NORM_EPS)
            ubuf[lanes(half * 128 + r * chunk, chunk, chunk), :] = (hid * inv * gain).astype(jnp.bfloat16)

    slot = 2 * yz + core
    zcopies = []
    for n, (off, size) in enumerate(parts):
        loads[n].wait()
        z = dot(ubuf[...], wbuf[:, off:off + size]).astype(jnp.bfloat16)
        zbuf[:, :, off:off + size] = z.reshape(4, 64, size)
        for k, (y, co, target) in enumerate(((1 - yz, core, ynbr), (1 - yz, 1 - core, far), (yz, 1 - core, partner))):
            zcopies.append(remote(zbuf.at[2 * y + co, :, pl.ds(off, size)], z_ref.at[slot, :, pl.ds(off, size)],
                                  zsend.at[n, k], zrecv.at[n, k], target))
            zcopies[-1].start()
    z_ref[slot] = zbuf[slot]
    hres_ref[...] = hx_ref[:, :, lanes(slot_columns(yz, core), 1024, 512)]
    for copy in copies:
        copy.wait_send()
    for copy in zcopies:
        copy.wait()


def project_qkv(h, gain, w_qkv):
    model, half = w_qkv.shape
    width = (half // 128 + 1) // 2 * 128
    h4 = h.reshape(2, 2, 128, h.shape[1])
    return pl.pallas_call(
        qkv_kernel,
        out_shape=(jax.ShapeDtypeStruct((4, 64, width), jnp.bfloat16),
                   jax.ShapeDtypeStruct((2, 128, model // 4), jnp.bfloat16)),
        in_specs=[pl.BlockSpec(memory_space=VMEM), pl.BlockSpec(memory_space=VMEM), pl.BlockSpec(memory_space=pl.ANY)],
        out_specs=(pl.BlockSpec(memory_space=VMEM), pl.BlockSpec(memory_space=VMEM)),
        scratch_shapes=[VMEM((2, 128, model), jnp.bfloat16), VMEM((model, width), jnp.bfloat16), VMEM((256, model), jnp.bfloat16),
                        VMEM((4, 64, width), jnp.bfloat16), DMA((2,)), DMA((7,)), DMA((7,)), DMA((2, 3)), DMA((2, 3))],
        compiler_params=pltpu.CompilerParams(collective_id=0, has_side_effects=True, vmem_limit_bytes=40 * MIB),
        name='qkv',
    )(h4, gain, w_qkv)


def attention_kernel(lens_ref, order_ref, z_ref, k_ref, v_ref, o_ref, ko_ref, vo_ref,
                     qs, kn, vn, os, kbuf, vbuf, sem, fsem, *, heads, group, depth, unit):
    seqs, length, dim = k_ref.shape
    tiles = (heads + 2) // 2
    split = tiles // 2
    groups = seqs // group
    sizes = length // unit

    def tile(t):
        y, local = t // tiles, t % tiles
        co = 1 if local >= split else 0
        first = (local - split * co) * dim
        return z_ref[2 * y + co, :, first:first + dim].astype(jnp.float32)

    def by_size(g, act):
        need = lens_ref[order_ref[g * group]] // unit + 1
        for size in range(1, sizes + 1):
            @pl.when(need == size)
            def _():
                act(size * unit)

    def fetch(g, rows):
        out = []
        for m in range(group):
            b = order_ref[g * group + m]
            s = lax.rem(g, depth) * group + m
            out.append(pltpu.make_async_copy(k_ref.at[b, pl.ds(0, rows)], kbuf.at[s, pl.ds(0, rows)], sem.at[0, s]))
            out.append(pltpu.make_async_copy(v_ref.at[b, pl.ds(0, rows)], vbuf.at[s, pl.ds(0, rows)], sem.at[1, s]))
        return out

    def flush(g):
        out = []
        for m in range(group):
            b = order_ref[g * group + m]
            s = lax.rem(g, depth) * group + m
            out.append(pltpu.make_async_copy(kbuf.at[s], ko_ref.at[b], fsem.at[0, s]))
            out.append(pltpu.make_async_copy(vbuf.at[s], vo_ref.at[b], fsem.at[1, s]))
        return out

    def arrive(g, begin):
        for copy in fetch(g, length):
            if begin:
                copy.start()
            else:
                copy.wait()

    for g in range(2):
        arrive(jnp.int32(g), True)
    for t in range(heads):
        qs[pl.ds(t, seqs, stride=heads), :] = tile(t)
    kn[...] = tile(heads)
    vn[...] = tile(heads + 1)

    @pl.loop(0, groups)
    def _(g):
        @pl.when(g >= depth - 2)
        def _():
            for copy in flush(g - (depth - 2)):
                copy.wait()

        @pl.when(g + 2 < groups)
        def _():
            arrive(g + 2, True)

        arrive(g, False)
        for m in range(group):
            b = order_ref[g * group + m]
            s = lax.rem(g, depth) * group + m
            last = lens_ref[b]
            base = pl.multiple_of(last // 16 * 16, 16)
            row = lax.broadcasted_iota(jnp.int32, (16, dim), 0) == last - base
            for buf, new in ((kbuf, kn), (vbuf, vn)):
                old = buf[s, pl.ds(base, 16), :].astype(jnp.float32)
                buf[s, pl.ds(base, 16), :] = jnp.where(row, new[pl.ds(b, 1), :], old).astype(jnp.bfloat16)

        for copy in flush(g):
            copy.start()

        def act(rows):
            scores = []
            for m in range(group):
                b = order_ref[g * group + m]
                s = lax.rem(g, depth) * group + m
                q = qs[lanes(b * heads, heads, heads), :].astype(jnp.bfloat16)
                raw = lax.dot_general(q, kbuf[s, :rows], (((1,), (1,)), ((), ())), preferred_element_type=jnp.float32)
                seen = lax.broadcasted_iota(jnp.int32, (heads, rows), 1) <= lens_ref[b]
                scores.append(jnp.where(seen, raw * dim ** -0.5, -1e30))
            tops = [jnp.max(x, axis=1, keepdims=True) for x in scores]
            probs = [jnp.exp(x - top) for x, top in zip(scores, tops)]
            sums = [1.0 / jnp.sum(x, axis=1, keepdims=True) for x in probs]
            for m in range(group):
                b = order_ref[g * group + m]
                s = lax.rem(g, depth) * group + m
                os[lanes(b * heads, heads, heads), :] = dot((probs[m] * sums[m]).astype(jnp.bfloat16), vbuf[s, :rows])

        by_size(g, act)

    for t in range(heads):
        o_ref[:, t * dim:(t + 1) * dim] = os[pl.ds(t, seqs, stride=heads), :].astype(jnp.bfloat16)

    @pl.loop(groups - (depth - 2), groups)
    def _(g):
        for copy in flush(g):
            copy.wait()


def by_length(lens):
    ids = jnp.arange(lens.shape[0])
    ahead = (lens[None, :] > lens[:, None]) | ((lens[None, :] == lens[:, None]) & (ids[None, :] < ids[:, None]))
    rank = jnp.sum(ahead.astype(jnp.int32), axis=1)
    order = jnp.sum(jnp.where(rank[None, :] == ids[:, None], ids[None, :], 0), axis=1).astype(jnp.int32)
    return order


def attend(lens, order, z, k_cache, v_cache):
    seqs, length, dim = k_cache.shape
    heads = 32
    group, depth, unit = GROUP, DEPTH, 256
    anywhere = pl.BlockSpec(memory_space=pl.ANY)
    vmem = pl.BlockSpec(memory_space=VMEM)
    smem = pl.BlockSpec(memory_space=pltpu.SMEM)
    return pl.pallas_call(
        functools.partial(attention_kernel, heads=heads, group=group, depth=depth, unit=unit),
        out_shape=(jax.ShapeDtypeStruct((seqs, heads * dim), jnp.bfloat16),
                   jax.ShapeDtypeStruct(k_cache.shape, k_cache.dtype), jax.ShapeDtypeStruct(v_cache.shape, v_cache.dtype)),
        in_specs=[smem, smem, vmem, anywhere, anywhere],
        out_specs=(vmem, anywhere, anywhere),
        scratch_shapes=[VMEM((seqs * heads, dim), jnp.float32), VMEM((seqs, dim), jnp.float32),
                        VMEM((seqs, dim), jnp.float32), VMEM((seqs * heads, dim), jnp.float32),
                        VMEM((group * depth, length, dim), jnp.bfloat16), VMEM((group * depth, length, dim), jnp.bfloat16),
                        DMA((2, group * depth)), DMA((2, group * depth))],
        compiler_params=pltpu.CompilerParams(vmem_limit_bytes=50 * MIB),
        name='attention',
    )(lens, order, z, k_cache, v_cache)


def mlp_kernel(o_ref, hres, gain_ref, wo_ref, gu_ref, wd_ref, out_ref,
               og, wo, ys, yr, own, h1, inv_ref, ubuf, ue, gub, gacc, mbuf, wd, ps, pr, acc, fs, fr, xs, st,
               s_wo, s_gu, s_wd, send, recv, ysend, yrecv, hsend, hrecv, asend, arecv, osend, orecv, ssend, srecv,
               psend, precv, fsend, frecv, xsend, xrecv):
    yz, chip, core = place()
    half = wo_ref.shape[0]
    model = wo_ref.shape[1]
    inner = gu_ref.shape[2] // 2
    tiles = inner // 512
    ynbr, xnbr, partner = device(1 - yz, chip, core), device(yz, 1 - chip, core), device(yz, chip, 1 - core)
    far = device(1 - yz, chip, 1 - core)

    wo_copies = [pltpu.make_async_copy(wo_ref.at[:, lanes(core * half + n * 512, 512, 512)], wo.at[n], s_wo.at[n])
                 for n in range(4)]

    def place_of(p):
        y = jnp.where(p < 4, yz, 1 - yz)
        return (p % 4) // 2 * 4 + 2 * y + p % 2

    def gu_copies(q):
        s = lax.rem(q, 3)
        n = lax.rem(q, tiles)
        return [pltpu.make_async_copy(
            gu_ref.at[lanes(place_of(q // tiles * 4 + r) * 512, 512, 512), :, lanes(core * inner + n * 512, 512, 512)],
            gub.at[s, pl.ds(r * 512, 512)], s_gu.at[s, r]) for r in range(4)]

    def column(t):
        k = t // 2
        y = jnp.where(k < 2, 1 - yz, yz)
        ch = jnp.where(k % 2 == 0, 1 - chip, chip)
        co = jnp.where(t % 2 == 0, 1 - core, core)
        return 2 * (2 * ch + co) + y

    def wd_copies(t):
        s = lax.rem(t, 3)
        rows = inner // 2
        return [pltpu.make_async_copy(wd_ref.at[lanes(core * inner + r * rows, rows, rows), lanes(column(t) * 512, 512, 512)],
                                      wd.at[s, pl.ds(r * rows, rows)], s_wd.at[s, r]) for r in range(2)]

    for copy in wo_copies:
        copy.start()
    greet((ynbr, xnbr, partner, far))

    slot = 2 * yz + core
    to_y = remote(o_ref.at[:, lanes((1 - yz) * half, half, 512)], og.at[slot], send.at[0], recv.at[0], ynbr)
    to_y.start()
    to_p = remote(o_ref.at[:, lanes(yz * half, half, 512)], og.at[slot], send.at[1], recv.at[1], partner)
    to_p.start()
    og[slot] = o_ref[:, lanes(yz * half, half, 512)]
    for q in range(3):
        for copy in gu_copies(jnp.int32(q)):
            copy.start()
    for t in range(3):
        for copy in wd_copies(jnp.int32(t)):
            copy.start()
    for copy in wo_copies:
        copy.wait()
    to_y.wait_recv()
    theirs = og.at[2 * (1 - yz) + core]
    onward = remote(theirs, theirs, send.at[2], recv.at[2], partner)
    onward.start()
    to_p.wait_recv()
    onward.wait_recv()

    def y_copy(e):
        return remote(ys.at[e], yr.at[e], ysend.at[e], yrecv.at[e], ynbr)

    @pl.loop(0, 2)
    def _(e):
        ys[e] = dot(og[...].reshape(256, half), wo[2 * (1 - yz) + e]).astype(jnp.bfloat16)
        y_copy(e).start()

    @pl.loop(0, 2)
    def _(e):
        own[e] = dot(og[...].reshape(256, half), wo[2 * yz + e])

    first = 4 * core + 2 * yz

    def h_send(e):
        return remote(h1.at[first + e], h1.at[first + e], hsend.at[e], hrecv.at[e], partner)

    def a_send(e):
        return remote(h1.at[first + e], h1.at[first + e], asend.at[e], arecv.at[e], ynbr)

    def onto(e):
        there = h1.at[4 * core + 2 * (1 - yz) + e]
        return remote(there, there, osend.at[e], orecv.at[e], partner)

    power = jnp.zeros((256, 1), jnp.float32)
    for e in range(2):
        y_copy(e).wait_recv()
        res = hres[:, :, e * 512:(e + 1) * 512].reshape(256, 512).astype(jnp.float32)
        hid = (res + (own[e] + yr[e].astype(jnp.float32))).astype(jnp.bfloat16)
        h1[first + e] = hid
        h_send(e).start()
        hid = hid.astype(jnp.float32)
        power += jnp.sum(hid * hid, axis=1, keepdims=True)

    at_lane = lax.broadcasted_iota(jnp.int32, (32, 8, 128), 2) == lax.broadcasted_iota(jnp.int32, (32, 8, 128), 0)
    st[slot] = jnp.sum(jnp.where(at_lane, power.reshape(32, 8, 1), 0.0), axis=0)
    stats = [remote(st.at[slot], st.at[slot], ssend.at[k], srecv.at[k], target)
             for k, target in enumerate((ynbr, far, partner))]
    for copy in stats:
        copy.start()
    for e in range(2):
        a_send(e).start()
    for copy in stats:
        copy.wait_recv()
    total = (st[0] + st[1]) + (st[2] + st[3])
    power = jnp.sum(jnp.where(at_lane, total[None], 0.0), axis=2, keepdims=True).reshape(256, 1)
    inv_ref[...] = jnp.broadcast_to(lax.rsqrt(power / model + NORM_EPS), (256, 128))

    at = lax.broadcasted_iota(jnp.int32, (128, 512), 1)
    spread = (at % 256 == 2 * lax.broadcasted_iota(jnp.int32, (128, 512), 0) + at // 256).astype(jnp.bfloat16)

    def prepare(p):
        b = place_of(p)
        gain = gain_ref[:, lanes(b * 512, 512, 512)].astype(jnp.float32)
        ubuf[...] = (h1[b].astype(jnp.float32) * inv_ref[:, :1] * gain).astype(jnp.bfloat16)
        for q in range(4):
            wide = dot(ubuf[:, q * 128:(q + 1) * 128], spread).astype(jnp.bfloat16)
            ue[:256, lanes(p * 1024 + q * 256, 256, 256)] = wide[:, :256]
            ue[256:, lanes(p * 1024 + q * 256, 256, 256)] = wide[:, 256:]

    for e in range(2):
        h_send(e).wait_recv()

    @pl.loop(0, 4)
    def _(p):
        prepare(p)

    def more(q):
        @pl.when(q + 3 < 2 * tiles)
        def _():
            for copy in gu_copies(q + 3):
                copy.start()

    @pl.loop(0, tiles)
    def _(n):
        @pl.when((n == 2) | (n == 4))
        def _():
            a_send(n // 2 - 1).wait_recv()
            onto(n // 2 - 1).start()

        for copy in gu_copies(n):
            copy.wait()
        gacc[n] = dot(ue[:, :model], gub.at[lax.rem(n, 3)].reshape(model, 512)[...])
        more(n)

    for e in range(2):
        onto(e).wait_recv()

    @pl.loop(4, 8)
    def _(p):
        prepare(p)

    @pl.loop(0, tiles)
    def _(n):
        q = n + tiles
        for copy in gu_copies(q):
            copy.wait()
        both = gacc[n] + dot(ue[:, model:], gub.at[lax.rem(q, 3)].reshape(model, 512)[...])
        more(q)
        gate = both[:256].astype(jnp.bfloat16).astype(jnp.float32)
        up = both[256:].astype(jnp.bfloat16).astype(jnp.float32)
        mbuf[:, lanes(n * 512, 512, 512)] = (gate * jax.nn.sigmoid(gate) * up).astype(jnp.bfloat16)

    def p_copy(k):
        return remote(ps.at[k], pr.at[k], psend.at[k], precv.at[k], partner)

    def f_copy(k):
        return remote(fs.at[k], fr.at[k], fsend.at[k], frecv.at[k], ynbr)

    x_copy = remote(xs, out_ref.at[:, chip], xsend.at[0], xrecv.at[0], xnbr)

    @pl.loop(0, 4)
    def _(k):
        for side in range(2):
            t = 2 * k + side
            s = lax.rem(t, 3)
            for copy in wd_copies(t):
                copy.wait()
            part = dot(mbuf[...], wd[s])

            @pl.when(t + 3 < 8)
            def _():
                for copy in wd_copies(t + 3):
                    copy.start()

            if side == 0:
                ps[k] = part.astype(jnp.bfloat16)
                p_copy(k).start()
            else:
                acc[...] = part
        p_copy(k).wait_recv()
        acc[...] += pr[k].astype(jnp.float32)

        @pl.when(k < 2)
        def _():
            fs[k] = acc[...].astype(jnp.bfloat16)
            f_copy(k).start()

        @pl.when(k >= 2)
        def _():
            f_copy(k - 2).wait_recv()
            total = acc[...] + fr[k - 2].astype(jnp.float32)
            final = (h1[column(2 * k + 1)].astype(jnp.float32) + total).astype(jnp.bfloat16).reshape(2, 128, 512)

            @pl.when(k == 2)
            def _():
                xs[...] = final
                x_copy.start()

            @pl.when(k == 3)
            def _():
                out_ref[:, chip] = final

    x_copy.wait()
    for copy in (to_y, to_p, onward):
        copy.wait_send()

    for copy in stats:
        copy.wait_send()
    for n in range(4):
        p_copy(n).wait_send()
    for n in range(2):
        for copy in (y_copy(n), h_send(n), a_send(n), onto(n), f_copy(n)):
            copy.wait_send()


def mlp(o, hres, gain, w_out, w_gate_up, w_down):
    half, model = w_out.shape
    inner = w_gate_up.shape[2] // 2
    anywhere = pl.BlockSpec(memory_space=pl.ANY)
    vmem = pl.BlockSpec(memory_space=VMEM)
    bf16 = jnp.bfloat16
    out = pl.pallas_call(
        mlp_kernel,
        out_shape=jax.ShapeDtypeStruct((2, 2, 128, 512), bf16),
        in_specs=[vmem, vmem, vmem, anywhere, anywhere, anywhere],
        out_specs=vmem,
        scratch_shapes=[
            VMEM((4, 64, half), bf16), VMEM((4, half, 512), bf16),
            VMEM((2, 256, 512), bf16), VMEM((2, 256, 512), bf16), VMEM((2, 256, 512), jnp.float32), VMEM((8, 256, 512), bf16),
            VMEM((256, 128), jnp.float32), VMEM((256, 512), bf16), VMEM((512, 2 * model), bf16),
            VMEM((3, half, 2, 512), bf16), VMEM((inner // 512, 512, 512), jnp.float32),
            VMEM((256, inner), bf16), VMEM((3, inner, 512), bf16),
            VMEM((4, 256, 512), bf16), VMEM((4, 256, 512), bf16), VMEM((256, 512), jnp.float32),
            VMEM((2, 256, 512), bf16), VMEM((2, 256, 512), bf16), VMEM((2, 128, 512), bf16), VMEM((4, 8, 128), jnp.float32),
            DMA((4,)), DMA((3, 4)), DMA((3, 2)),
            DMA((3,)), DMA((3,)), DMA((2,)), DMA((2,)), DMA((2,)), DMA((2,)), DMA((2,)), DMA((2,)), DMA((2,)), DMA((2,)),
            DMA((3,)), DMA((3,)),
            DMA((4,)), DMA((4,)), DMA((2,)), DMA((2,)), DMA((1,)), DMA((1,)),
        ],
        compiler_params=pltpu.CompilerParams(collective_id=1, has_side_effects=True, vmem_limit_bytes=60 * MIB),
        name='mlp',
    )(o, hres, gain, w_out, w_gate_up, w_down)
    return out.reshape(512, 512)


def move_kernel(h_ref, out_ref, sem):
    copy = pltpu.make_async_copy(h_ref, out_ref, sem)
    copy.start()
    copy.wait()


def move(hidden):
    return pl.pallas_call(
        move_kernel,
        out_shape=jax.ShapeDtypeStruct(hidden.shape, hidden.dtype),
        in_specs=[pl.BlockSpec(memory_space=VMEM)],
        out_specs=pl.BlockSpec(memory_space=pl.ANY),
        scratch_shapes=[DMA],
        name='move',
    )(hidden)


def solution(mesh):
    batch_axes = ('replica', 'yz', 'x')
    hidden_spec = P('replica', ('x', 'yz'))
    cache_spec = P(None, batch_axes, None, None)

    def local_step(hidden, seq_lens, attn_gain, mlp_gain, w_qkv, w_out, w_gate_up, w_down, k_cache, v_cache):
        k_layers = []
        v_layers = []
        for layer in range(w_qkv.shape[0]):
            z, hres = project_qkv(hidden, attn_gain[layer:layer + 1], w_qkv[layer])
            o, k_upd, v_upd = attend(seq_lens, by_length(seq_lens), z, k_cache[layer], v_cache[layer])
            k_layers.append(k_upd)
            v_layers.append(v_upd)
            hidden = mlp(o, hres, mlp_gain[layer:layer + 1], w_out[layer], w_gate_up[layer], w_down[layer])
        return move(hidden), jnp.stack(k_layers), jnp.stack(v_layers)

    return jax.shard_map(
        local_step,
        mesh=mesh,
        in_specs=(hidden_spec, P(batch_axes), P(None, None), P(None, None), P(None, None, 'yz'), P(None, 'yz', None),
                  P(None, None, None, 'yz'), P(None, 'yz', None), cache_spec, cache_spec),
        out_specs=(hidden_spec, cache_spec, cache_spec),
        check_vma=False)
```

time: 175 us -> 167 us (0.954)
  Pallas kernels: 168 us -> 161 us
    pallas_call x1, Pallas kernels: 92.2 us -> 85.1 us  [mlp(): pl.pallas_call(mlp_kernel, out_shape=jax.ShapeDtypeStruct((2, 2, 128, 512...]
    unnamed x11 -> x10, local copies, waits for them, and re-layouts: 5.09 us -> 3.97 us
    pallas_call x1 -> x2, Pallas kernels: 46.7 us -> 46 us  [the longest x1 44.1 us: attend(): pl.pallas_call(functools.partial(attention_kernel, heads=heads, group=gro...]
where the time goes in v2:
time: 167 us; the launch traced here: 166 us
  Pallas kernels  161 us (96%)
  local copies, waits for them, and re-layouts  3.97 us (2%)
    pallas_call x1, Pallas kernels, mlp(): pl.pallas_call(mlp_kernel, out_shape=jax.ShapeDtypeStruct((2, 2, 128, 512...  85.1 us
    pallas_call x1, Pallas kernels, attend(): pl.pallas_call(functools.partial(attention_kernel, heads=heads, group=gro...  44.1 us
    pallas_call x1, Pallas kernels, project_qkv(): pl.pallas_call(qkv_kernel, out_shape=(jax.ShapeDtypeStruct((4, 64, width)...  29.6 us
    unnamed x10, local copies, waits for them, and re-layouts  3.97 us

profile of v2, /device:TPU:0, one launch (start us, length us, event | category | flops | bytes accessed | tf_op | source)
XLA Modules:
  0.0 166.5 jit_solution(725417956182572598)
XLA Ops:
  0.6 0.9 convert_reduce_fusion
  1.5 0.1 select_reduce_fusion.order_ref
  1.7 0.0 copy-start.2
  1.7 1.0 copy-done.2
  2.7 0.0 copy-start.3
  2.7 0.7 copy-done.3
  3.4 29.6 %qkv.1 = (bf16[4,64,1152]{2,1,0:T(8,128)(2,1)S(1)}, bf16[2,128,1024]{2,1,0:T(8,128)(2,1)S(1)}) custom-call(bf16[2,2,128,512]{3,2,1,0:T(8,128)(2,1)S(1)} %bitcast.10, bf16[1,4096]{1,0:T(2,128)(2,1)S(1)} %copy-done.3, bf16[4096,2176]{1,0:T(8,128)(2,1)} %bitcast.14), custom_call_target="tpu_custom_call" | custom-call | tf_op jit(solution)/shard_map/qkv/pallas_call | solution.py:117
  33.0 0.0 copy-start
  33.0 0.8 copy-done
  33.8 0.0 copy-start.4
  33.8 0.7 copy-done.4
  34.5 44.1 %attention.1 = (bf16[64,4096]{1,0:T(8,128)(2,1)S(1)}, bf16[64,2048,128]{2,1,0:T(8,128)(2,1)}, bf16[64,2048,128]{2,1,0:T(8,128)(2,1)}) custom-call(s32[64]{0:T(128)S(1)} %copy-done.4, s32[64]{0:T(128)S(1)} %select_reduce_fusion.order_ref, bf16[4,64,1152]{2,1,0:T(8,128)(2,1)S(1)} %get-tuple-element.8.z_ref, bf16[64,2048,128]{2,1,0:T(8,128)(2,1)} %bitcast.12, ...), custom_call_target="tpu_custom_call" | custom-call | tf_op jit(solution)/shard_map/attention/pallas_call | solution.py:251
  78.6 0.0 copy-start.1
  78.6 0.8 copy-done.1
  79.4 85.1 %mlp.1 = bf16[2,2,128,512]{3,2,1,0:T(8,128)(2,1)} custom-call(bf16[64,4096]{1,0:T(8,128)(2,1)} %copy-done.1, bf16[2,128,1024]{2,1,0:T(8,128)(2,1)} %copy-done, bf16[1,4096]{1,0:T(2,128)(2,1)} %gain_ref.3, bf16[2048,4096]{1,0:T(8,128)(2,1)} %bitcast.15, bf16[4096,2,7168]{2,1,0:T(2,128)(2,1)} %bitcast.5.gu_ref, bf16[7168,4096]{1,0:T(8,128)(2,1)} %bitcast.11), custom_call_target="tpu_custom_call" | custom-call | tf_op jit(solution)/shard_map/mlp/pallas_call | solution.py:502
  164.5 1.8 %move.1 = bf16[512,512]{1,0:T(8,128)(2,1)} custom-call(bf16[512,512]{1,0:T(8,128)(2,1)} %bitcast.16), custom_call_target="tpu_custom_call" | custom-call | tf_op jit(solution)/shard_map/move/pallas_call | solution.py:533
Async XLA Ops:
  1.7 1.1 copy-start.2
  2.7 0.7 copy-start.3
  33.0 0.8 copy-start
  33.8 0.7 copy-start.4
  78.6 0.8 copy-start.1

commit v3 on v2

--- a/solution.py
+++ b/solution.py
@@ -11,6 +11,7 @@
 MESH = pl.DeviceIdType.MESH
 MIB = 1 << 20
 GROUP, DEPTH = 4, 4
+EARLY = 16
 VMEM = pltpu.VMEM
 DMA = pltpu.SemaphoreType.DMA
 
@@ -49,9 +50,63 @@
     return jnp.dot(a, b, preferred_element_type=jnp.float32)
 
 
-def qkv_kernel(h_ref, gain_ref, w_ref, z_ref, hres_ref, hx_ref, wbuf, ubuf, zbuf, w_sem, send, recv, zsend, zrecv):
+def early_kernel(order_ref, k_ref, v_ref, ko_ref, vo_ref, kbuf, vbuf, isem, osem, *, count, slots, ahead):
+    def moves(t, into):
+        s = lax.rem(t, slots)
+        b = order_ref[(t // GROUP * 4 + 2) * GROUP + lax.rem(t, GROUP)]
+        if into:
+            return (pltpu.make_async_copy(k_ref.at[b], kbuf.at[s], isem.at[0, s]),
+                    pltpu.make_async_copy(v_ref.at[b], vbuf.at[s], isem.at[1, s]))
+        return (pltpu.make_async_copy(kbuf.at[s], ko_ref.at[b], osem.at[0, s]),
+                pltpu.make_async_copy(vbuf.at[s], vo_ref.at[b], osem.at[1, s]))
+
+    @pl.loop(0, ahead)
+    def _(t):
+        for copy in moves(t, True):
+            copy.start()
+
+    @pl.loop(0, count)
+    def _(t):
+        @pl.when(t + ahead < count)
+        def _():
+            @pl.when(t + ahead >= slots)
+            def _():
+                for copy in moves(t + ahead - slots, False):
+                    copy.wait()
+            for copy in moves(t + ahead, True):
+                copy.start()
+
+        for copy in moves(t, True):
+            copy.wait()
+        for copy in moves(t, False):
+            copy.start()
+
+    @pl.loop(max(count - slots, 0), count)
+    def _(t):
+        for copy in moves(t, False):
+            copy.wait()
+
+
+def copy_early(order, k_cache, v_cache):
+    anywhere = pl.BlockSpec(memory_space=pl.ANY)
+    slots, ahead = 16, 8
+    return pl.pallas_call(
+        functools.partial(early_kernel, count=EARLY, slots=slots, ahead=ahead),
+        out_shape=tuple(jax.ShapeDtypeStruct(x.shape, x.dtype) for x in (k_cache, v_cache)),
+        in_specs=[pl.BlockSpec(memory_space=pltpu.SMEM), anywhere, anywhere],
+        out_specs=(anywhere, anywhere),
+        scratch_shapes=[VMEM((slots,) + k_cache.shape[1:], jnp.bfloat16), VMEM((slots,) + k_cache.shape[1:], jnp.bfloat16),
+                        DMA((2, slots)), DMA((2, slots))],
+        cost_estimate=pl.CostEstimate(flops=10 ** 11, bytes_accessed=4 * EARLY * k_cache[0].size * 2, transcendentals=0),
+        compiler_params=pltpu.CompilerParams(vmem_limit_bytes=40 * MIB),
+        name='copy_early',
+    )(order, k_cache, v_cache)
+
+
+def qkv_kernel(own_ref, by_ref, bx_ref, bd_ref, gain_ref, w_ref, _, z_ref, hres_ref, hx_ref, wbuf, ubuf, zbuf,
+               w_sem, send, recv, zsend, zrecv):
     yz, chip, core = place()
-    cols = h_ref.shape[-1]
+    cols = own_ref.shape[-1]
     width = z_ref.shape[-1]
     parts = ((0, 512), (512, width - 512))
     step = w_ref.shape[1] - width
@@ -61,27 +116,19 @@
         loads.append(pltpu.make_async_copy(w_ref.at[:, lanes(core * step + off, size)],
                                            wbuf.at[:, pl.ds(off, size)], w_sem.at[n]))
         loads[-1].start()
-    ynbr, xnbr = device(1 - yz, chip, core), device(yz, 1 - chip, core)
-    diag, partner = device(1 - yz, 1 - chip, core), device(yz, chip, 1 - core)
+    ynbr, partner = device(1 - yz, chip, core), device(yz, chip, 1 - core)
     far = device(1 - yz, chip, 1 - core)
-    greet((ynbr, xnbr, diag, partner, far))
-
-    def block(y, ch, co):
-        return hx_ref.at[:, :, lanes((2 * (2 * ch + co) + y) * cols, cols, 512)]
-
-    mine = block(yz, chip, core)
+    greet((ynbr, partner, far))
     copies = []
-    for k, (src, target) in enumerate(((1 - chip, diag), (chip, ynbr), (1 - chip, xnbr), (chip, partner))):
-        copies.append(remote(h_ref.at[:, src], mine, send.at[k], recv.at[k], target))
+    blocks = ((own_ref, yz, chip), (by_ref, 1 - yz, chip), (bx_ref, yz, 1 - chip), (bd_ref, 1 - yz, 1 - chip))
+    for k, (ref, y, ch) in enumerate(blocks):
+        here = lanes((2 * (2 * ch + core) + y) * cols, cols, 512)
+        copies.append(remote(ref, hx_ref.at[:, :, here], send.at[k], recv.at[k], partner))
         copies[-1].start()
-    hx_ref[:, :, lanes((2 * (2 * chip + core) + yz) * cols, cols, 512)] = h_ref[:, chip]
-    arrivals = ((1, block(1 - yz, chip, core)), (2, block(yz, 1 - chip, core)), (0, block(1 - yz, 1 - chip, core)))
-    for k, (which, ref) in enumerate(arrivals):
-        copies[which].wait_recv()
-        copies.append(remote(ref, ref, send.at[4 + k], recv.at[4 + k], partner))
-        copies[-1].start()
-    for k in (3, 4, 5, 6):
-        copies[k].wait_recv()
+    for ref, y, ch in blocks:
+        hx_ref[:, :, lanes((2 * (2 * ch + core) + y) * cols, cols, 512)] = ref[...]
+    for copy in copies:
+        copy.wait_recv()
 
     gain = gain_ref[...].astype(jnp.float32)
     chunk = 32
@@ -110,24 +157,25 @@
         copy.wait()
 
 
-def project_qkv(h, gain, w_qkv):
+def project_qkv(blocks, gain, w_qkv, after):
     model, half = w_qkv.shape
     width = (half // 128 + 1) // 2 * 128
-    h4 = h.reshape(2, 2, 128, h.shape[1])
+    vmem = pl.BlockSpec(memory_space=VMEM)
+    anywhere = pl.BlockSpec(memory_space=pl.ANY)
     return pl.pallas_call(
         qkv_kernel,
         out_shape=(jax.ShapeDtypeStruct((4, 64, width), jnp.bfloat16),
                    jax.ShapeDtypeStruct((2, 128, model // 4), jnp.bfloat16)),
-        in_specs=[pl.BlockSpec(memory_space=VMEM), pl.BlockSpec(memory_space=VMEM), pl.BlockSpec(memory_space=pl.ANY)],
+        in_specs=[vmem, vmem, vmem, vmem, vmem, anywhere, anywhere],
         out_specs=(pl.BlockSpec(memory_space=VMEM), pl.BlockSpec(memory_space=VMEM)),
         scratch_shapes=[VMEM((2, 128, model), jnp.bfloat16), VMEM((model, width), jnp.bfloat16), VMEM((256, model), jnp.bfloat16),
-                        VMEM((4, 64, width), jnp.bfloat16), DMA((2,)), DMA((7,)), DMA((7,)), DMA((2, 3)), DMA((2, 3))],
+                        VMEM((4, 64, width), jnp.bfloat16), DMA((2,)), DMA((4,)), DMA((4,)), DMA((2, 3)), DMA((2, 3))],
         compiler_params=pltpu.CompilerParams(collective_id=0, has_side_effects=True, vmem_limit_bytes=40 * MIB),
         name='qkv',
-    )(h4, gain, w_qkv)
-
-
-def attention_kernel(lens_ref, order_ref, z_ref, k_ref, v_ref, o_ref, ko_ref, vo_ref,
+    )(*blocks, gain, w_qkv, after)
+
+
+def attention_kernel(lens_ref, order_ref, z_ref, k_ref, v_ref, _, __, o_ref, ko_ref, vo_ref,
                      qs, kn, vn, os, kbuf, vbuf, sem, fsem, *, heads, group, depth, unit):
     seqs, length, dim = k_ref.shape
     tiles = (heads + 2) // 2
@@ -157,21 +205,38 @@
             out.append(pltpu.make_async_copy(v_ref.at[b, pl.ds(0, rows)], vbuf.at[s, pl.ds(0, rows)], sem.at[1, s]))
         return out
 
-    def flush(g):
-        out = []
-        for m in range(group):
-            b = order_ref[g * group + m]
-            s = lax.rem(g, depth) * group + m
-            out.append(pltpu.make_async_copy(kbuf.at[s], ko_ref.at[b], fsem.at[0, s]))
-            out.append(pltpu.make_async_copy(vbuf.at[s], vo_ref.at[b], fsem.at[1, s]))
-        return out
+    def flush(g, act):
+        def tail(rows_of):
+            for m in range(group):
+                b = order_ref[g * group + m]
+                s = lax.rem(g, depth) * group + m
+                rows = rows_of(b)
+                act(pltpu.make_async_copy(kbuf.at[s, rows], ko_ref.at[b, rows], fsem.at[0, s]))
+                act(pltpu.make_async_copy(vbuf.at[s, rows], vo_ref.at[b, rows], fsem.at[1, s]))
+
+        @pl.when(lax.rem(g, 4) != 2)
+        def _():
+            tail(lambda b: pl.ds(0, length))
+
+        @pl.when(lax.rem(g, 4) == 2)
+        def _():
+            tail(lambda b: lanes(lens_ref[b] // 16 * 16, 16, 16))
 
     def arrive(g, begin):
-        for copy in fetch(g, length):
-            if begin:
-                copy.start()
-            else:
-                copy.wait()
+        def act(rows):
+            for copy in fetch(g, rows):
+                if begin:
+                    copy.start()
+                else:
+                    copy.wait()
+
+        @pl.when(lax.rem(g, 4) != 2)
+        def _():
+            act(length)
+
+        @pl.when(lax.rem(g, 4) == 2)
+        def _():
+            by_size(g, act)
 
     for g in range(2):
         arrive(jnp.int32(g), True)
@@ -184,8 +249,7 @@
     def _(g):
         @pl.when(g >= depth - 2)
         def _():
-            for copy in flush(g - (depth - 2)):
-                copy.wait()
+            flush(g - (depth - 2), lambda copy: copy.wait())
 
         @pl.when(g + 2 < groups)
         def _():
@@ -202,8 +266,7 @@
                 old = buf[s, pl.ds(base, 16), :].astype(jnp.float32)
                 buf[s, pl.ds(base, 16), :] = jnp.where(row, new[pl.ds(b, 1), :], old).astype(jnp.bfloat16)
 
-        for copy in flush(g):
-            copy.start()
+        flush(g, lambda copy: copy.start())
 
         def act(rows):
             scores = []
@@ -229,19 +292,22 @@
 
     @pl.loop(groups - (depth - 2), groups)
     def _(g):
-        for copy in flush(g):
-            copy.wait()
+        flush(g, lambda copy: copy.wait())
 
 
 def by_length(lens):
-    ids = jnp.arange(lens.shape[0])
+    seqs = lens.shape[0]
+    ids = jnp.arange(seqs)
     ahead = (lens[None, :] > lens[:, None]) | ((lens[None, :] == lens[:, None]) & (ids[None, :] < ids[:, None]))
     rank = jnp.sum(ahead.astype(jnp.int32), axis=1)
-    order = jnp.sum(jnp.where(rank[None, :] == ids[:, None], ids[None, :], 0), axis=1).astype(jnp.int32)
-    return order
-
-
-def attend(lens, order, z, k_cache, v_cache):
+    late = (seqs - EARLY) // GROUP
+    place_in = rank // GROUP
+    place_in = jnp.where(place_in < late, place_in + (place_in + 1) // 3, 4 * (place_in - late) + 2)
+    place_in = place_in * GROUP + rank % GROUP
+    return jnp.sum(jnp.where(place_in[None, :] == ids[:, None], ids[None, :], 0), axis=1).astype(jnp.int32)
+
+
+def attend(lens, order, z, k_cache, v_cache, k_out, v_out):
     seqs, length, dim = k_cache.shape
     heads = 32
     group, depth, unit = GROUP, DEPTH, 256
@@ -252,15 +318,16 @@
         functools.partial(attention_kernel, heads=heads, group=group, depth=depth, unit=unit),
         out_shape=(jax.ShapeDtypeStruct((seqs, heads * dim), jnp.bfloat16),
                    jax.ShapeDtypeStruct(k_cache.shape, k_cache.dtype), jax.ShapeDtypeStruct(v_cache.shape, v_cache.dtype)),
-        in_specs=[smem, smem, vmem, anywhere, anywhere],
+        in_specs=[smem, smem, vmem, anywhere, anywhere, anywhere, anywhere],
         out_specs=(vmem, anywhere, anywhere),
+        input_output_aliases={5: 1, 6: 2},
         scratch_shapes=[VMEM((seqs * heads, dim), jnp.float32), VMEM((seqs, dim), jnp.float32),
                         VMEM((seqs, dim), jnp.float32), VMEM((seqs * heads, dim), jnp.float32),
                         VMEM((group * depth, length, dim), jnp.bfloat16), VMEM((group * depth, length, dim), jnp.bfloat16),
                         DMA((2, group * depth)), DMA((2, group * depth))],
         compiler_params=pltpu.CompilerParams(vmem_limit_bytes=50 * MIB),
         name='attention',
-    )(lens, order, z, k_cache, v_cache)
+    )(lens, order, z, k_cache, v_cache, k_out, v_out)
 
 
 def mlp_kernel(o_ref, hres, gain_ref, wo_ref, gu_ref, wd_ref, out_ref,
@@ -549,8 +616,17 @@
         k_layers = []
         v_layers = []
         for layer in range(w_qkv.shape[0]):
-            z, hres = project_qkv(hidden, attn_gain[layer:layer + 1], w_qkv[layer])
-            o, k_upd, v_upd = attend(seq_lens, by_length(seq_lens), z, k_cache[layer], v_cache[layer])
+            order = by_length(seq_lens)
+            rows = hidden.reshape(2, 2, 128, hidden.shape[1])
+            chip = lax.axis_index('x') // 2
+            own = lax.dynamic_index_in_dim(rows, chip, 1, keepdims=False)
+            other = lax.dynamic_index_in_dim(rows, 1 - chip, 1, keepdims=False)
+            by = lax.ppermute(own, 'yz', [(0, 1), (1, 0)])
+            bx = lax.ppermute(other, 'x', [(j, j ^ 2) for j in range(4)])
+            bd = lax.ppermute(other, ('yz', 'x'), [(j, j ^ 6) for j in range(8)])
+            k_upd, v_upd = copy_early(order, k_cache[layer], v_cache[layer])
+            z, hres = project_qkv((own, by, bx, bd), attn_gain[layer:layer + 1], w_qkv[layer], k_upd)
+            o, k_upd, v_upd = attend(seq_lens, order, z, k_cache[layer], v_cache[layer], k_upd, v_upd)
             k_layers.append(k_upd)
             v_layers.append(v_upd)
             hidden = mlp(o, hres, mlp_gain[layer:layer + 1], w_out[layer], w_gate_up[layer], w_down[layer])

time: 167 us -> 161 us (0.964); the launches traced: 166 us -> 162 us
  Pallas kernels: 161 us -> 153 us
  starting transfers between devices: 0 us -> 4.91 us
    pallas_call x1, Pallas kernels: 29.6 us -> 14.2 us  [project_qkv(): pl.pallas_call(qkv_kernel, out_shape=(jax.ShapeDtypeStruct((4, 64, width)...]
    pallas_call x0 -> x1, Pallas kernels: none -> 13.2 us  [copy_early(): pl.pallas_call(functools.partial(early_kernel, count=EARLY, slots=slots,...]
    pallas_call x1, Pallas kernels: 44.1 us -> 35.5 us  [attend(): pl.pallas_call(functools.partial(attention_kernel, heads=heads, group=gro...]
    ppermute x0 -> x3, starting transfers between devices: none -> 4.91 us  [the longest x1 4.32 us: local_step(): bd = lax.ppermute(other, ('yz', 'x'), [(j, j ^ 6) for j in range(8)])]
    pallas_call x1, Pallas kernels: 85.1 us -> 87.9 us  [mlp(): pl.pallas_call(mlp_kernel, out_shape=jax.ShapeDtypeStruct((2, 2, 128, 512...]
    unnamed x10 -> x8, local copies, waits for them, and re-layouts: 3.97 us -> 1.58 us
  transfers between devices with their start and end apart: 0 -> 3, of which waited for: 0 -> 0; matrix products, arithmetic and copies ran while one was open for 0% -> 1% of each run, Pallas kernels for 0% -> 8%
where the time goes in v3:
time: 161 us; the launch traced here: 162 us
  Pallas kernels  153 us (95%)
  starting transfers between devices  4.91 us (3%)
  local copies, waits for them, and re-layouts  2.65 us (2%)
    pallas_call x1, Pallas kernels, mlp(): pl.pallas_call(mlp_kernel, out_shape=jax.ShapeDtypeStruct((2, 2, 128, 512...  87.9 us
    pallas_call x1, Pallas kernels, attend(): pl.pallas_call(functools.partial(attention_kernel, heads=heads, group=gro...  35.5 us
    pallas_call x1, Pallas kernels, project_qkv(): pl.pallas_call(qkv_kernel, out_shape=(jax.ShapeDtypeStruct((4, 64, width)...  14.2 us
    pallas_call x1, Pallas kernels, copy_early(): pl.pallas_call(functools.partial(early_kernel, count=EARLY, slots=slots,...  13.2 us
    ppermute x1, starting transfers between devices, local_step(): bd = lax.ppermute(other, ('yz', 'x'), [(j, j ^ 6) for j in range(8)])  4.32 us
  transfers between devices with their start and end apart: 3, of which 0 were waited for; matrix products, arithmetic and copies ran while one was open for 1% of the time, Pallas kernels for 8%

profile of v3, /device:TPU:0, one launch (start us, length us, event | category | flops | bytes accessed | tf_op | source)
XLA Modules:
  0.0 162.2 jit_solution(361855278811244577)
XLA Ops:
  0.7 1.1 dynamic-slice_bitcast_fusion
  1.7 4.3 %collective-permute-start.2 = (bf16[2,128,512]{2,1,0:T(8,128)(2,1)S(1)}, bf16[2,128,512]{2,1,0:T(8,128)(2,1)S(1)}, u32[]{:S(2)}, u32[]{:S(2)}) collective-permute-start(bf16[2,128,512]{2,1,0:T(8,128)(2,1)S(1)} %get-tuple-element.17), channel_id=1, source_target_pairs={{0,6},{1,7},{2,4},{3,5},{4,2},{5,3},{6,0},{7,1}} | collective-permute-start | bytes 786440 | tf_op jit(solution)/shard_map/ppermute | solution.py:626
  6.0 0.5 collective-permute-start.1
  6.6 0.1 collective-permute-start
  6.6 0.9 convert_reduce_fusion
  7.6 0.1 select_reduce_fusion.order_ref
  7.7 0.0 copy-start.2
  7.7 13.2 %copy_early.1 = (bf16[64,2048,128]{2,1,0:T(8,128)(2,1)}, bf16[64,2048,128]{2,1,0:T(8,128)(2,1)}) custom-call(s32[64]{0:T(128)S(1)} %select_reduce_fusion.order_ref, bf16[64,2048,128]{2,1,0:T(8,128)(2,1)} %bitcast.20, bf16[64,2048,128]{2,1,0:T(8,128)(2,1)} %bitcast.22), custom_call_target="tpu_custom_call" | custom-call | flops 99999997952 | bytes 33554432 | tf_op jit(solution)/shard_map/copy_early/pallas_call | solution.py:93
  20.9 0.0 copy-start.3
  20.9 0.0 collective-permute-done.2.bd_ref
  20.9 0.0 collective-permute-done.1.bx_ref
  20.9 0.0 collective-permute-done.by_ref
  20.9 0.0 copy-done.2
  21.0 14.2 %qkv.1 = (bf16[4,64,1152]{2,1,0:T(8,128)(2,1)S(1)}, bf16[2,128,1024]{2,1,0:T(8,128)(2,1)S(1)}) custom-call(bf16[2,128,512]{2,1,0:T(8,128)(2,1)S(1)} %get-tuple-element.18.own_ref, bf16[2,128,512]{2,1,0:T(8,128)(2,1)S(1)} %collective-permute-done.by_ref, bf16[2,128,512]{2,1,0:T(8,128)(2,1)S(1)} %collective-permute-done.1.bx_ref, ...), custom_call_target="tpu_custom_call" | custom-call | tf_op jit(solution)/shard_map/qkv/pallas_call | solution.py:165
  35.1 0.0 copy-start
  35.1 0.8 copy-done
  35.9 0.0 copy-done.3
  35.9 35.5 %attention.1 = (bf16[64,4096]{1,0:T(8,128)(2,1)S(1)}, bf16[64,2048,128]{2,1,0:T(8,128)(2,1)}, bf16[64,2048,128]{2,1,0:T(8,128)(2,1)}) custom-call(s32[64]{0:T(128)S(1)} %copy-done.3, s32[64]{0:T(128)S(1)} %select_reduce_fusion.order_ref, bf16[4,64,1152]{2,1,0:T(8,128)(2,1)S(1)} %get-tuple-element.11.z_ref, ...), custom_call_target="tpu_custom_call", output_to_operand_aliasing={{1}: (5, {}), {2}: (6, {})} | custom-call | tf_op jit(solution)/shard_map/attention/pallas_call | solution.py:317
  71.4 0.0 copy-start.1
  71.4 0.8 copy-done.1
  72.2 87.9 %mlp.1 = bf16[2,2,128,512]{3,2,1,0:T(8,128)(2,1)} custom-call(bf16[64,4096]{1,0:T(8,128)(2,1)} %copy-done.1, bf16[2,128,1024]{2,1,0:T(8,128)(2,1)} %copy-done, bf16[1,4096]{1,0:T(2,128)(2,1)} %gain_ref.3, bf16[2048,4096]{1,0:T(8,128)(2,1)} %bitcast.26, bf16[4096,2,7168]{2,1,0:T(2,128)(2,1)} %bitcast.7.gu_ref, bf16[7168,4096]{1,0:T(8,128)(2,1)} %bitcast.19), custom_call_target="tpu_custom_call" | custom-call | tf_op jit(solution)/shard_map/mlp/pallas_call | solution.py:569
  160.2 1.8 %move.1 = bf16[512,512]{1,0:T(8,128)(2,1)} custom-call(bf16[512,512]{1,0:T(8,128)(2,1)} %bitcast.27), custom_call_target="tpu_custom_call" | custom-call | tf_op jit(solution)/shard_map/move/pallas_call | solution.py:600
  (1 shorter events, 0.0 us)
Async XLA Ops:
  1.7 19.2 %collective-permute-start.2 = (bf16[2,128,512]{2,1,0:T(8,128)(2,1)S(1)}, bf16[2,128,512]{2,1,0:T(8,128)(2,1)S(1)}, u32[]{:S(2)}, u32[]{:S(2)}) collective-permute-start(bf16[2,128,512]{2,1,0:T(8,128)(2,1)S(1)} %get-tuple-element.17), channel_id=1, source_target_pairs={{0,6},{1,7},{2,4},{3,5},{4,2},{5,3},{6,0},{7,1}} | collective-permute-start | bytes 786440 | tf_op jit(solution)/shard_map/ppermute | solution.py:626
  6.0 14.9 %collective-permute-start.1 = (bf16[2,128,512]{2,1,0:T(8,128)(2,1)S(1)}, bf16[2,128,512]{2,1,0:T(8,128)(2,1)S(1)}, u32[]{:S(2)}, u32[]{:S(2)}) collective-permute-start(bf16[2,128,512]{2,1,0:T(8,128)(2,1)S(1)} %get-tuple-element.17), channel_id=1, source_target_pairs={{0,2},{1,3},{2,0},{3,1},{4,6},{5,7},{6,4},{7,5}} | collective-permute-start | bytes 786440 | tf_op jit(solution)/shard_map/ppermute | solution.py:625
  6.6 14.4 %collective-permute-start = (bf16[2,128,512]{2,1,0:T(8,128)(2,1)S(1)}, bf16[2,128,512]{2,1,0:T(8,128)(2,1)S(1)}, u32[]{:S(2)}, u32[]{:S(2)}) collective-permute-start(bf16[2,128,512]{2,1,0:T(8,128)(2,1)S(1)} %get-tuple-element.18.own_ref), channel_id=1, source_target_pairs={{0,4},{4,0},{1,5},{5,1},{2,6},{6,2},{3,7},{7,3}} | collective-permute-start | bytes 786440 | tf_op jit(solution)/shard_map/ppermute | solution.py:624
  7.7 13.2 %copy-start.2 = (bf16[1,4096]{1,0:T(2,128)(2,1)S(1)}, bf16[1,4096]{1,0:T(2,128)(2,1)}, u32[]{:S(2)}) copy-start(bf16[1,4096]{1,0:T(2,128)(2,1)} %gain_ref.2) | copy-start | bytes 24580
  20.9 15.0 %copy-start.3 = (s32[64]{0:T(128)S(1)}, s32[64]{0:T(128)}, u32[]{:S(2)}) copy-start(s32[64]{0:T(128)} %lens_ref.1) | copy-start | bytes 772
  35.1 0.8 copy-start
  71.4 0.8 copy-start.1

commit v4 on v3

--- a/solution.py
+++ b/solution.py
@@ -12,8 +12,13 @@
 MIB = 1 << 20
 GROUP, DEPTH = 4, 4
 EARLY = 16
+COLS, ROWS, LANE, PAIR, SEQS = 512, 256, 128, 1024, 64
 VMEM = pltpu.VMEM
 DMA = pltpu.SemaphoreType.DMA
+ONE = DMA((1,))
+TWO = DMA((2,))
+THREE = DMA((3,))
+FOUR = DMA((4,))
 
 
 def place():
@@ -108,7 +113,7 @@
     yz, chip, core = place()
     cols = own_ref.shape[-1]
     width = z_ref.shape[-1]
-    parts = ((0, 512), (512, width - 512))
+    parts = ((0, COLS), (COLS, width - COLS))
     step = w_ref.shape[1] - width
     model = hx_ref.shape[-1]
     loads = []
@@ -122,35 +127,35 @@
     copies = []
     blocks = ((own_ref, yz, chip), (by_ref, 1 - yz, chip), (bx_ref, yz, 1 - chip), (bd_ref, 1 - yz, 1 - chip))
     for k, (ref, y, ch) in enumerate(blocks):
-        here = lanes((2 * (2 * ch + core) + y) * cols, cols, 512)
+        here = lanes((2 * (2 * ch + core) + y) * cols, cols, COLS)
         copies.append(remote(ref, hx_ref.at[:, :, here], send.at[k], recv.at[k], partner))
         copies[-1].start()
     for ref, y, ch in blocks:
-        hx_ref[:, :, lanes((2 * (2 * ch + core) + y) * cols, cols, 512)] = ref[...]
+        hx_ref[:, :, lanes((2 * (2 * ch + core) + y) * cols, cols, COLS)] = ref[...]
     for copy in copies:
         copy.wait_recv()
 
     gain = gain_ref[...].astype(jnp.float32)
     chunk = 32
     for half in range(2):
-        @pl.loop(0, 128 // chunk)
+        @pl.loop(0, LANE // chunk)
         def _(r):
             hid = hx_ref[half, lanes(r * chunk, chunk, chunk), :].astype(jnp.float32)
             inv = lax.rsqrt(jnp.sum(hid * hid, axis=1, keepdims=True) / model + NORM_EPS)
-            ubuf[lanes(half * 128 + r * chunk, chunk, chunk), :] = (hid * inv * gain).astype(jnp.bfloat16)
+            ubuf[lanes(half * LANE + r * chunk, chunk, chunk), :] = (hid * inv * gain).astype(jnp.bfloat16)
 
     slot = 2 * yz + core
     zcopies = []
     for n, (off, size) in enumerate(parts):
         loads[n].wait()
         z = dot(ubuf[...], wbuf[:, off:off + size]).astype(jnp.bfloat16)
-        zbuf[:, :, off:off + size] = z.reshape(4, 64, size)
+        zbuf[:, :, off:off + size] = z.reshape(4, SEQS, size)
         for k, (y, co, target) in enumerate(((1 - yz, core, ynbr), (1 - yz, 1 - core, far), (yz, 1 - core, partner))):
             zcopies.append(remote(zbuf.at[2 * y + co, :, pl.ds(off, size)], z_ref.at[slot, :, pl.ds(off, size)],
                                   zsend.at[n, k], zrecv.at[n, k], target))
             zcopies[-1].start()
     z_ref[slot] = zbuf[slot]
-    hres_ref[...] = hx_ref[:, :, lanes(slot_columns(yz, core), 1024, 512)]
+    hres_ref[...] = hx_ref[:, :, lanes(slot_columns(yz, core), PAIR, COLS)]
     for copy in copies:
         copy.wait_send()
     for copy in zcopies:
@@ -159,17 +164,17 @@
 
 def project_qkv(blocks, gain, w_qkv, after):
     model, half = w_qkv.shape
-    width = (half // 128 + 1) // 2 * 128
+    width = (half // LANE + 1) // 2 * LANE
     vmem = pl.BlockSpec(memory_space=VMEM)
     anywhere = pl.BlockSpec(memory_space=pl.ANY)
     return pl.pallas_call(
         qkv_kernel,
-        out_shape=(jax.ShapeDtypeStruct((4, 64, width), jnp.bfloat16),
-                   jax.ShapeDtypeStruct((2, 128, model // 4), jnp.bfloat16)),
+        out_shape=(jax.ShapeDtypeStruct((4, SEQS, width), jnp.bfloat16),
+                   jax.ShapeDtypeStruct((2, LANE, model // 4), jnp.bfloat16)),
         in_specs=[vmem, vmem, vmem, vmem, vmem, anywhere, anywhere],
         out_specs=(pl.BlockSpec(memory_space=VMEM), pl.BlockSpec(memory_space=VMEM)),
-        scratch_shapes=[VMEM((2, 128, model), jnp.bfloat16), VMEM((model, width), jnp.bfloat16), VMEM((256, model), jnp.bfloat16),
-                        VMEM((4, 64, width), jnp.bfloat16), DMA((2,)), DMA((4,)), DMA((4,)), DMA((2, 3)), DMA((2, 3))],
+        scratch_shapes=[VMEM((2, LANE, model), jnp.bfloat16), VMEM((model, width), jnp.bfloat16), VMEM((ROWS, model), jnp.bfloat16),
+                        VMEM((4, SEQS, width), jnp.bfloat16), TWO, FOUR, FOUR, DMA((2, 3)), DMA((2, 3))],
         compiler_params=pltpu.CompilerParams(collective_id=0, has_side_effects=True, vmem_limit_bytes=40 * MIB),
         name='qkv',
     )(*blocks, gain, w_qkv, after)
@@ -310,7 +315,7 @@
 def attend(lens, order, z, k_cache, v_cache, k_out, v_out):
     seqs, length, dim = k_cache.shape
     heads = 32
-    group, depth, unit = GROUP, DEPTH, 256
+    group, depth, unit = GROUP, DEPTH, ROWS
     anywhere = pl.BlockSpec(memory_space=pl.ANY)
     vmem = pl.BlockSpec(memory_space=VMEM)
     smem = pl.BlockSpec(memory_space=pltpu.SMEM)
@@ -338,11 +343,11 @@
     half = wo_ref.shape[0]
     model = wo_ref.shape[1]
     inner = gu_ref.shape[2] // 2
-    tiles = inner // 512
+    tiles = inner // COLS
     ynbr, xnbr, partner = device(1 - yz, chip, core), device(yz, 1 - chip, core), device(yz, chip, 1 - core)
     far = device(1 - yz, chip, 1 - core)
 
-    wo_copies = [pltpu.make_async_copy(wo_ref.at[:, lanes(core * half + n * 512, 512, 512)], wo.at[n], s_wo.at[n])
+    wo_copies = [pltpu.make_async_copy(wo_ref.at[:, lanes(core * half + n * COLS, COLS, COLS)], wo.at[n], s_wo.at[n])
                  for n in range(4)]
 
     def place_of(p):
@@ -353,8 +358,8 @@
         s = lax.rem(q, 3)
         n = lax.rem(q, tiles)
         return [pltpu.make_async_copy(
-            gu_ref.at[lanes(place_of(q // tiles * 4 + r) * 512, 512, 512), :, lanes(core * inner + n * 512, 512, 512)],
-            gub.at[s, pl.ds(r * 512, 512)], s_gu.at[s, r]) for r in range(4)]
+            gu_ref.at[lanes(place_of(q // tiles * 4 + r) * COLS, COLS, COLS), :, lanes(core * inner + n * COLS, COLS, COLS)],
+            gub.at[s, pl.ds(r * COLS, COLS)], s_gu.at[s, r]) for r in range(4)]
 
     def column(t):
         k = t // 2
@@ -366,7 +371,7 @@
     def wd_copies(t):
         s = lax.rem(t, 3)
         rows = inner // 2
-        return [pltpu.make_async_copy(wd_ref.at[lanes(core * inner + r * rows, rows, rows), lanes(column(t) * 512, 512, 512)],
+        return [pltpu.make_async_copy(wd_ref.at[lanes(core * inner + r * rows, rows, rows), lanes(column(t) * COLS, COLS, COLS)],
                                       wd.at[s, pl.ds(r * rows, rows)], s_wd.at[s, r]) for r in range(2)]
 
     for copy in wo_copies:
@@ -374,11 +379,11 @@
     greet((ynbr, xnbr, partner, far))
 
     slot = 2 * yz + core
-    to_y = remote(o_ref.at[:, lanes((1 - yz) * half, half, 512)], og.at[slot], send.at[0], recv.at[0], ynbr)
+    to_y = remote(o_ref.at[:, lanes((1 - yz) * half, half, COLS)], og.at[slot], send.at[0], recv.at[0], ynbr)
     to_y.start()
-    to_p = remote(o_ref.at[:, lanes(yz * half, half, 512)], og.at[slot], send.at[1], recv.at[1], partner)
+    to_p = remote(o_ref.at[:, lanes(yz * half, half, COLS)], og.at[slot], send.at[1], recv.at[1], partner)
     to_p.start()
-    og[slot] = o_ref[:, lanes(yz * half, half, 512)]
+    og[slot] = o_ref[:, lanes(yz * half, half, COLS)]
     for q in range(3):
         for copy in gu_copies(jnp.int32(q)):
             copy.start()
@@ -399,12 +404,12 @@
 
     @pl.loop(0, 2)
     def _(e):
-        ys[e] = dot(og[...].reshape(256, half), wo[2 * (1 - yz) + e]).astype(jnp.bfloat16)
+        ys[e] = dot(og[...].reshape(ROWS, half), wo[2 * (1 - yz) + e]).astype(jnp.bfloat16)
         y_copy(e).start()
 
     @pl.loop(0, 2)
     def _(e):
-        own[e] = dot(og[...].reshape(256, half), wo[2 * yz + e])
+        own[e] = dot(og[...].reshape(ROWS, half), wo[2 * yz + e])
 
     first = 4 * core + 2 * yz
 
@@ -418,17 +423,17 @@
         there = h1.at[4 * core + 2 * (1 - yz) + e]
         return remote(there, there, osend.at[e], orecv.at[e], partner)
 
-    power = jnp.zeros((256, 1), jnp.float32)
+    power = jnp.zeros((ROWS, 1), jnp.float32)
     for e in range(2):
         y_copy(e).wait_recv()
-        res = hres[:, :, e * 512:(e + 1) * 512].reshape(256, 512).astype(jnp.float32)
+        res = hres[:, :, e * COLS:(e + 1) * COLS].reshape(ROWS, COLS).astype(jnp.float32)
         hid = (res + (own[e] + yr[e].astype(jnp.float32))).astype(jnp.bfloat16)
         h1[first + e] = hid
         h_send(e).start()
         hid = hid.astype(jnp.float32)
         power += jnp.sum(hid * hid, axis=1, keepdims=True)
 
-    at_lane = lax.broadcasted_iota(jnp.int32, (32, 8, 128), 2) == lax.broadcasted_iota(jnp.int32, (32, 8, 128), 0)
+    at_lane = lax.broadcasted_iota(jnp.int32, (32, 8, LANE), 2) == lax.broadcasted_iota(jnp.int32, (32, 8, LANE), 0)
     st[slot] = jnp.sum(jnp.where(at_lane, power.reshape(32, 8, 1), 0.0), axis=0)
     stats = [remote(st.at[slot], st.at[slot], ssend.at[k], srecv.at[k], target)
              for k, target in enumerate((ynbr, far, partner))]
@@ -439,20 +444,20 @@
     for copy in stats:
         copy.wait_recv()
     total = (st[0] + st[1]) + (st[2] + st[3])
-    power = jnp.sum(jnp.where(at_lane, total[None], 0.0), axis=2, keepdims=True).reshape(256, 1)
-    inv_ref[...] = jnp.broadcast_to(lax.rsqrt(power / model + NORM_EPS), (256, 128))
-
-    at = lax.broadcasted_iota(jnp.int32, (128, 512), 1)
-    spread = (at % 256 == 2 * lax.broadcasted_iota(jnp.int32, (128, 512), 0) + at // 256).astype(jnp.bfloat16)
+    power = jnp.sum(jnp.where(at_lane, total[None], 0.0), axis=2, keepdims=True).reshape(ROWS, 1)
+    inv_ref[...] = jnp.broadcast_to(lax.rsqrt(power / model + NORM_EPS), (ROWS, LANE))
+
+    at = lax.broadcasted_iota(jnp.int32, (LANE, COLS), 1)
+    spread = (at % ROWS == 2 * lax.broadcasted_iota(jnp.int32, (LANE, COLS), 0) + at // ROWS).astype(jnp.bfloat16)
 
     def prepare(p):
         b = place_of(p)
-        gain = gain_ref[:, lanes(b * 512, 512, 512)].astype(jnp.float32)
+        gain = gain_ref[:, lanes(b * COLS, COLS, COLS)].astype(jnp.float32)
         ubuf[...] = (h1[b].astype(jnp.float32) * inv_ref[:, :1] * gain).astype(jnp.bfloat16)
         for q in range(4):
-            wide = dot(ubuf[:, q * 128:(q + 1) * 128], spread).astype(jnp.bfloat16)
-            ue[:256, lanes(p * 1024 + q * 256, 256, 256)] = wide[:, :256]
-            ue[256:, lanes(p * 1024 + q * 256, 256, 256)] = wide[:, 256:]
+            wide = dot(ubuf[:, q * LANE:(q + 1) * LANE], spread).astype(jnp.bfloat16)
+            ue[:ROWS, lanes(p * PAIR + q * ROWS, ROWS, ROWS)] = wide[:, :ROWS]
+            ue[ROWS:, lanes(p * PAIR + q * ROWS, ROWS, ROWS)] = wide[:, ROWS:]
 
     for e in range(2):
         h_send(e).wait_recv()
@@ -476,7 +481,7 @@
 
         for copy in gu_copies(n):
             copy.wait()
-        gacc[n] = dot(ue[:, :model], gub.at[lax.rem(n, 3)].reshape(model, 512)[...])
+        gacc[n] = dot(ue[:, :model], gub.at[lax.rem(n, 3)].reshape(model, COLS)[...])
         more(n)
 
     for e in range(2):
@@ -491,11 +496,11 @@
         q = n + tiles
         for copy in gu_copies(q):
             copy.wait()
-        both = gacc[n] + dot(ue[:, model:], gub.at[lax.rem(q, 3)].reshape(model, 512)[...])
+        both = gacc[n] + dot(ue[:, model:], gub.at[lax.rem(q, 3)].reshape(model, COLS)[...])
         more(q)
-        gate = both[:256].astype(jnp.bfloat16).astype(jnp.float32)
-        up = both[256:].astype(jnp.bfloat16).astype(jnp.float32)
-        mbuf[:, lanes(n * 512, 512, 512)] = (gate * jax.nn.sigmoid(gate) * up).astype(jnp.bfloat16)
+        gate = both[:ROWS].astype(jnp.bfloat16).astype(jnp.float32)
+        up = both[ROWS:].astype(jnp.bfloat16).astype(jnp.float32)
+        mbuf[:, lanes(n * COLS, COLS, COLS)] = (gate * jax.nn.sigmoid(gate) * up).astype(jnp.bfloat16)
 
     def p_copy(k):
         return remote(ps.at[k], pr.at[k], psend.at[k], precv.at[k], partner)
@@ -536,7 +541,7 @@
         def _():
             f_copy(k - 2).wait_recv()
             total = acc[...] + fr[k - 2].astype(jnp.float32)
-            final = (h1[column(2 * k + 1)].astype(jnp.float32) + total).astype(jnp.bfloat16).reshape(2, 128, 512)
+            final = (h1[column(2 * k + 1)].astype(jnp.float32) + total).astype(jnp.bfloat16).reshape(2, LANE, COLS)
 
             @pl.when(k == 2)
             def _():
@@ -568,26 +573,26 @@
     bf16 = jnp.bfloat16
     out = pl.pallas_call(
         mlp_kernel,
-        out_shape=jax.ShapeDtypeStruct((2, 2, 128, 512), bf16),
+        out_shape=jax.ShapeDtypeStruct((2, 2, LANE, COLS), bf16),
         in_specs=[vmem, vmem, vmem, anywhere, anywhere, anywhere],
         out_specs=vmem,
         scratch_shapes=[
-            VMEM((4, 64, half), bf16), VMEM((4, half, 512), bf16),
-            VMEM((2, 256, 512), bf16), VMEM((2, 256, 512), bf16), VMEM((2, 256, 512), jnp.float32), VMEM((8, 256, 512), bf16),
-            VMEM((256, 128), jnp.float32), VMEM((256, 512), bf16), VMEM((512, 2 * model), bf16),
-            VMEM((3, half, 2, 512), bf16), VMEM((inner // 512, 512, 512), jnp.float32),
-            VMEM((256, inner), bf16), VMEM((3, inner, 512), bf16),
-            VMEM((4, 256, 512), bf16), VMEM((4, 256, 512), bf16), VMEM((256, 512), jnp.float32),
-            VMEM((2, 256, 512), bf16), VMEM((2, 256, 512), bf16), VMEM((2, 128, 512), bf16), VMEM((4, 8, 128), jnp.float32),
-            DMA((4,)), DMA((3, 4)), DMA((3, 2)),
-            DMA((3,)), DMA((3,)), DMA((2,)), DMA((2,)), DMA((2,)), DMA((2,)), DMA((2,)), DMA((2,)), DMA((2,)), DMA((2,)),
-            DMA((3,)), DMA((3,)),
-            DMA((4,)), DMA((4,)), DMA((2,)), DMA((2,)), DMA((1,)), DMA((1,)),
+            VMEM((4, SEQS, half), bf16), VMEM((4, half, COLS), bf16),
+            *(VMEM((2, ROWS, COLS), bf16),) * 2, VMEM((2, ROWS, COLS), jnp.float32), VMEM((8, ROWS, COLS), bf16),
+            VMEM((ROWS, LANE), jnp.float32), VMEM((ROWS, COLS), bf16), VMEM((COLS, 2 * model), bf16),
+            VMEM((3, half, 2, COLS), bf16), VMEM((inner // COLS, COLS, COLS), jnp.float32),
+            VMEM((ROWS, inner), bf16), VMEM((3, inner, COLS), bf16),
+            *(VMEM((4, ROWS, COLS), bf16),) * 2, VMEM((ROWS, COLS), jnp.float32),
+            *(VMEM((2, ROWS, COLS), bf16),) * 2, VMEM((2, LANE, COLS), bf16), VMEM((4, 8, LANE), jnp.float32),
+            FOUR, DMA((3, 4)), DMA((3, 2)),
+            THREE, THREE, TWO, TWO, TWO, TWO, TWO, TWO, TWO, TWO,
+            THREE, THREE,
+            FOUR, FOUR, TWO, TWO, ONE, ONE,
         ],
         compiler_params=pltpu.CompilerParams(collective_id=1, has_side_effects=True, vmem_limit_bytes=60 * MIB),
         name='mlp',
     )(o, hres, gain, w_out, w_gate_up, w_down)
-    return out.reshape(512, 512)
+    return out.reshape(COLS, COLS)
 
 
 def move_kernel(h_ref, out_ref, sem):
@@ -617,7 +622,7 @@
         v_layers = []
         for layer in range(w_qkv.shape[0]):
             order = by_length(seq_lens)
-            rows = hidden.reshape(2, 2, 128, hidden.shape[1])
+            rows = hidden.reshape(2, 2, LANE, hidden.shape[1])
             chip = lax.axis_index('x') // 2
             own = lax.dynamic_index_in_dim(rows, chip, 1, keepdims=False)
             other = lax.dynamic_index_in_dim(rows, 1 - chip, 1, keepdims=False)

time: 161 us -> 161 us (level)
  Pallas kernels: 153 us -> 151 us
where the time goes in v4:
time: 161 us
  Pallas kernels  151 us (94%)
  starting transfers between devices  4.91 us (3%)
  local copies, waits for them, and re-layouts  2.65 us (2%)
    pallas_call x1, Pallas kernels, mlp(): pl.pallas_call(mlp_kernel, out_shape=jax.ShapeDtypeStruct((2, 2, LANE, CO...  86.5 us
    pallas_call x1, Pallas kernels, attend(): pl.pallas_call(functools.partial(attention_kernel, heads=heads, group=gro...  35.7 us
    pallas_call x1, Pallas kernels, project_qkv(): pl.pallas_call(qkv_kernel, out_shape=(jax.ShapeDtypeStruct((4, SEQS, widt...  14.2 us
    pallas_call x1, Pallas kernels, copy_early(): pl.pallas_call(functools.partial(early_kernel, count=EARLY, slots=slots,...  13.2 us
    ppermute x1, starting transfers between devices, local_step(): bd = lax.ppermute(other, ('yz', 'x'), [(j, j ^ 6) for j in range(8)])  4.32 us
  transfers between devices with their start and end apart: 3, of which 0 were waited for; matrix products, arithmetic and copies ran while one was open for 1% of the time, Pallas kernels for 8%

profile of v4, /device:TPU:0, one launch (start us, length us, event | category | flops | bytes accessed | tf_op | source)
XLA Modules:
  0.0 160.9 jit_solution(361855278811244577)
XLA Ops:
  0.7 1.1 dynamic-slice_bitcast_fusion
  1.7 4.3 %collective-permute-start.2 = (bf16[2,128,512]{2,1,0:T(8,128)(2,1)S(1)}, bf16[2,128,512]{2,1,0:T(8,128)(2,1)S(1)}, u32[]{:S(2)}, u32[]{:S(2)}) collective-permute-start(bf16[2,128,512]{2,1,0:T(8,128)(2,1)S(1)} %get-tuple-element.17), channel_id=1, source_target_pairs={{0,6},{1,7},{2,4},{3,5},{4,2},{5,3},{6,0},{7,1}} | collective-permute-start | bytes 786440 | tf_op jit(solution)/shard_map/ppermute | solution.py:631
  6.0 0.5 collective-permute-start.1
  6.6 0.1 collective-permute-start
  6.6 0.9 convert_reduce_fusion
  7.6 0.1 select_reduce_fusion.order_ref
  7.7 0.0 copy-start.2
  7.7 13.2 %copy_early.1 = (bf16[64,2048,128]{2,1,0:T(8,128)(2,1)}, bf16[64,2048,128]{2,1,0:T(8,128)(2,1)}) custom-call(s32[64]{0:T(128)S(1)} %select_reduce_fusion.order_ref, bf16[64,2048,128]{2,1,0:T(8,128)(2,1)} %bitcast.20, bf16[64,2048,128]{2,1,0:T(8,128)(2,1)} %bitcast.22), custom_call_target="tpu_custom_call" | custom-call | flops 99999997952 | bytes 33554432 | tf_op jit(solution)/shard_map/copy_early/pallas_call | solution.py:98
  20.9 0.0 copy-start.3
  20.9 0.0 collective-permute-done.2.bd_ref
  20.9 0.0 collective-permute-done.1.bx_ref
  20.9 0.0 collective-permute-done.by_ref
  20.9 0.0 copy-done.2
  21.0 14.2 %qkv.1 = (bf16[4,64,1152]{2,1,0:T(8,128)(2,1)S(1)}, bf16[2,128,1024]{2,1,0:T(8,128)(2,1)S(1)}) custom-call(bf16[2,128,512]{2,1,0:T(8,128)(2,1)S(1)} %get-tuple-element.18.own_ref, bf16[2,128,512]{2,1,0:T(8,128)(2,1)S(1)} %collective-permute-done.by_ref, bf16[2,128,512]{2,1,0:T(8,128)(2,1)S(1)} %collective-permute-done.1.bx_ref, ...), custom_call_target="tpu_custom_call" | custom-call | tf_op jit(solution)/shard_map/qkv/pallas_call | solution.py:170
  35.1 0.0 copy-start
  35.1 0.8 copy-done
  35.9 0.0 copy-done.3
  35.9 35.7 %attention.1 = (bf16[64,4096]{1,0:T(8,128)(2,1)S(1)}, bf16[64,2048,128]{2,1,0:T(8,128)(2,1)}, bf16[64,2048,128]{2,1,0:T(8,128)(2,1)}) custom-call(s32[64]{0:T(128)S(1)} %copy-done.3, s32[64]{0:T(128)S(1)} %select_reduce_fusion.order_ref, bf16[4,64,1152]{2,1,0:T(8,128)(2,1)S(1)} %get-tuple-element.11.z_ref, ...), custom_call_target="tpu_custom_call", output_to_operand_aliasing={{1}: (5, {}), {2}: (6, {})} | custom-call | tf_op jit(solution)/shard_map/attention/pallas_call | solution.py:322
  71.7 0.0 copy-start.1
  71.7 0.8 copy-done.1
  72.5 86.5 %mlp.1 = bf16[2,2,128,512]{3,2,1,0:T(8,128)(2,1)} custom-call(bf16[64,4096]{1,0:T(8,128)(2,1)} %copy-done.1, bf16[2,128,1024]{2,1,0:T(8,128)(2,1)} %copy-done, bf16[1,4096]{1,0:T(2,128)(2,1)} %gain_ref.3, bf16[2048,4096]{1,0:T(8,128)(2,1)} %bitcast.26, bf16[4096,2,7168]{2,1,0:T(2,128)(2,1)} %bitcast.7.gu_ref, bf16[7168,4096]{1,0:T(8,128)(2,1)} %bitcast.19), custom_call_target="tpu_custom_call" | custom-call | tf_op jit(solution)/shard_map/mlp/pallas_call | solution.py:574
  158.9 1.8 %move.1 = bf16[512,512]{1,0:T(8,128)(2,1)} custom-call(bf16[512,512]{1,0:T(8,128)(2,1)} %bitcast.27), custom_call_target="tpu_custom_call" | custom-call | tf_op jit(solution)/shard_map/move/pallas_call | solution.py:605
  (1 shorter events, 0.0 us)
Async XLA Ops:
  1.7 19.2 %collective-permute-start.2 = (bf16[2,128,512]{2,1,0:T(8,128)(2,1)S(1)}, bf16[2,128,512]{2,1,0:T(8,128)(2,1)S(1)}, u32[]{:S(2)}, u32[]{:S(2)}) collective-permute-start(bf16[2,128,512]{2,1,0:T(8,128)(2,1)S(1)} %get-tuple-element.17), channel_id=1, source_target_pairs={{0,6},{1,7},{2,4},{3,5},{4,2},{5,3},{6,0},{7,1}} | collective-permute-start | bytes 786440 | tf_op jit(solution)/shard_map/ppermute | solution.py:631
  6.0 14.9 %collective-permute-start.1 = (bf16[2,128,512]{2,1,0:T(8,128)(2,1)S(1)}, bf16[2,128,512]{2,1,0:T(8,128)(2,1)S(1)}, u32[]{:S(2)}, u32[]{:S(2)}) collective-permute-start(bf16[2,128,512]{2,1,0:T(8,128)(2,1)S(1)} %get-tuple-element.17), channel_id=1, source_target_pairs={{0,2},{1,3},{2,0},{3,1},{4,6},{5,7},{6,4},{7,5}} | collective-permute-start | bytes 786440 | tf_op jit(solution)/shard_map/ppermute | solution.py:630
  6.6 14.4 %collective-permute-start = (bf16[2,128,512]{2,1,0:T(8,128)(2,1)S(1)}, bf16[2,128,512]{2,1,0:T(8,128)(2,1)S(1)}, u32[]{:S(2)}, u32[]{:S(2)}) collective-permute-start(bf16[2,128,512]{2,1,0:T(8,128)(2,1)S(1)} %get-tuple-element.18.own_ref), channel_id=1, source_target_pairs={{0,4},{4,0},{1,5},{5,1},{2,6},{6,2},{3,7},{7,3}} | collective-permute-start | bytes 786440 | tf_op jit(solution)/shard_map/ppermute | solution.py:629
  7.7 13.2 %copy-start.2 = (bf16[1,4096]{1,0:T(2,128)(2,1)S(1)}, bf16[1,4096]{1,0:T(2,128)(2,1)}, u32[]{:S(2)}) copy-start(bf16[1,4096]{1,0:T(2,128)(2,1)} %gain_ref.2) | copy-start | bytes 24580
  20.9 15.0 %copy-start.3 = (s32[64]{0:T(128)S(1)}, s32[64]{0:T(128)}, u32[]{:S(2)}) copy-start(s32[64]{0:T(128)} %lens_ref.1) | copy-start | bytes 772
  35.1 0.8 copy-start
  71.7 0.8 copy-start.1
